TPU v7x, 8 devices: a whole 2x2x1 slice. The times are simulated.
8 devices in a mesh: rep: 1 (over z), dp: 2 (over y), sp: 4 (over x, core).
Axes of the slice: x: 2, y: 2, z: 1, core: 2. Of those that a mesh axis runs over, the one named last changes fastest.
Arguments:
- hidden: bfloat16 [128, 4096], P(('rep', 'dp'))
- w_query: bfloat16 [4096, 4096], replicated
- w_key: bfloat16 [4096, 256], replicated
- w_value: bfloat16 [4096, 256], replicated
- w_out: bfloat16 [4096, 4096], P('sp')
- k_cache: bfloat16 [128, 1024, 1, 256], P(('rep', 'dp'), 'sp')
- v_cache: bfloat16 [128, 1024, 1, 256], P(('rep', 'dp'), 'sp')
- write_pos: int32 [128], P(('rep', 'dp'))
- valid_len: int32 [128], P(('rep', 'dp'))
Outputs:
- output 1: bfloat16 [128, 4096], P(('rep', 'dp'))
- output 2: bfloat16 [128, 1024, 1, 256], P(('rep', 'dp'), 'sp')
- output 3: bfloat16 [128, 1024, 1, 256], P(('rep', 'dp'), 'sp')
All inputs are finite; a program needn't handle non-finite values.
Results may differ from a plain program's by a relative error of at most 0.00657726.
Values are sent between devices in bfloat16 or wider.
A program may use at most 1 GiB of HBM per device.

v0:
```python
import jax
import jax.numpy as jnp
from jax import lax
from jax.sharding import PartitionSpec as P

NEG_FLOOR = -1e30


def solution(mesh):
    row_spec = P(('rep', 'dp'), None)
    cache_spec = P(('rep', 'dp'), 'sp', None, None)
    len_spec = P(('rep', 'dp'))

    def local_step(hidden, w_query, w_key, w_value, w_out, k_cache, v_cache, write_pos, valid_len):
        num_rows, seq_local, kv_heads, head_dim = k_cache.shape
        num_heads = w_query.shape[1] // head_dim
        group_size = num_heads // kv_heads
        shard_idx = lax.axis_index('sp')
        query = jnp.dot(hidden, w_query, preferred_element_type=jnp.float32).astype(jnp.bfloat16)
        query = query.reshape(num_rows, kv_heads, group_size, head_dim)
        key_new = jnp.dot(hidden, w_key, preferred_element_type=jnp.float32).astype(jnp.bfloat16)
        value_new = jnp.dot(hidden, w_value, preferred_element_type=jnp.float32).astype(jnp.bfloat16)
        positions = shard_idx * seq_local + jnp.arange(seq_local, dtype=jnp.int32)
        at_pos = (positions[None, :] == write_pos[:, None])[:, :, None, None]
        k_next = jnp.where(at_pos, key_new.reshape(num_rows, 1, kv_heads, head_dim), k_cache)
        v_next = jnp.where(at_pos, value_new.reshape(num_rows, 1, kv_heads, head_dim), v_cache)
        scores = jnp.einsum('bkgd,bskd->bkgs', query, k_next, preferred_element_type=jnp.float32) * head_dim ** -0.5
        valid_mask = (positions[None, :] < valid_len[:, None])[:, None, None, :]
        scores = jnp.where(valid_mask, scores, -jnp.inf)
        local_max = jnp.maximum(jnp.max(scores, axis=-1), NEG_FLOOR)
        weights = jnp.exp(scores - local_max[..., None])
        local_sum = jnp.sum(weights, axis=-1)
        local_acc = jnp.einsum('bkgs,bskd->bkgd', weights.astype(jnp.bfloat16), v_next, preferred_element_type=jnp.float32)
        global_max = lax.pmax(local_max, 'sp')
        rescale = jnp.exp(local_max - global_max)
        packed = jnp.concatenate([local_acc * rescale[..., None], (local_sum * rescale)[..., None]], axis=-1)
        packed = lax.psum(packed, 'sp')
        attention = (packed[..., :head_dim] / packed[..., head_dim:]).astype(jnp.bfloat16)
        attention = attention.reshape(num_rows, num_heads * head_dim)
        out_rows = w_out.shape[0]
        attn_mine = lax.dynamic_slice_in_dim(attention, shard_idx * out_rows, out_rows, axis=1)
        partial_out = jnp.dot(attn_mine, w_out, preferred_element_type=jnp.float32)
        attn_out = lax.psum(partial_out, 'sp').astype(jnp.bfloat16)
        return attn_out, k_next, v_next

    return jax.shard_map(local_step, mesh=mesh, in_specs=(row_spec, P(), P(), P(), P('sp', None), cache_spec, cache_spec, len_spec, len_spec), out_specs=(row_spec, cache_spec, cache_spec), check_vma=False)
```

profile of v0, /device:TPU:0, one launch (start us, length us, event | category | flops | bytes accessed | tf_op | source)
XLA Modules:
  0.0 142.4 jit_solution(9912607417767368675)
XLA Ops:
  7.2 0.0 copy-start
  7.2 0.0 all-reduce.3.cloned.1.call-start
  7.2 1.5 %copy-done = bf16[4096,256]{1,0:T(8,128)(2,1)S(1)} copy-done((bf16[4096,256]{1,0:T(8,128)(2,1)S(1)}, bf16[4096,256]{1,0:T(8,128)(2,1)}, u32[]{:S(2)}) %copy-start) | copy-done | bytes 2097176
  8.8 1.5 %convolution_convert_fusion.2 = bf16[64,256]{1,0:T(8,128)(2,1)S(1)} fusion(bf16[64,4096]{1,0:T(8,128)(2,1)} %param.9, bf16[4096,256]{1,0:T(8,128)(2,1)S(1)} %copy-done), kind=kOutput, calls=%fused_computation.13 | convolution fusion | flops 134234112 | bytes 2654208 | tf_op jit(solution)/shard_map/dot_general | solution.py:21
  10.3 0.0 slice-start
  10.3 2.4 %convolution_convert_fusion.1 = bf16[64,256]{1,0:T(8,128)(2,1)S(1)} fusion(bf16[64,4096]{1,0:T(8,128)(2,1)} %param.9, bf16[4096,256]{1,0:T(8,128)(2,1)} %param.12), kind=kOutput, calls=%fused_computation.12 | convolution fusion | flops 134234112 | bytes 2654208 | tf_op jit(solution)/shard_map/dot_general | solution.py:22
  12.6 0.0 copy-start.3
  12.7 0.0 copy-start.4
  12.7 0.0 slice-start.1
  12.7 16.8 %convolution_convert_fusion = bf16[64,4096]{1,0:T(8,128)(2,1)S(1)} fusion(bf16[64,4096]{1,0:T(8,128)(2,1)} %param.9, bf16[4096,4096]{1,0:T(8,128)(2,1)} %param.10), kind=kOutput, calls=%fused_computation.6 | convolution fusion | flops 2147745792 | bytes 34603008 | tf_op jit(solution)/shard_map/dot_general | solution.py:19
  29.5 0.1 copy.24
  29.6 0.0 copy-done.3
  29.6 0.0 copy-done.4
  29.6 0.1 broadcast_compare_fusion.1
  29.7 0.0 slice-done
  29.7 8.0 %broadcast_select_fusion = (bf16[64,256,1,256]{3,1,2,0:T(8,128)(2,1)}, bf16[64,256,1,256]{3,1,2,0:T(8,128)(2,1)S(1)}) fusion(bf16[64,256,1,256]{3,1,2,0:T(8,128)(2,1)S(1)} %bitcast.47, pred[64,256]{1,0:T(8,128)(4,1)S(1)} %get-tuple-element.10, bf16[64,256]{1,0:T(8,128)(2,1)S(1)} %convolution_convert_fusion.1, bf16[64,256,1,256]{3,1,2,0:T(8,128)(2,1)} %param.14, ...), kind=kLoop, calls=%fused_computation.4 | loop fusion | flops 8388608 | bytes 33636352 | tf_op jit(solution)/shard_map/jit(_where)/select_n | solution.py:26
  37.7 3.4 %copy-done.2 = bf16[64,256,1,256]{3,1,2,0:T(8,128)(2,1)} copy-done((bf16[64,256,1,256]{3,1,2,0:T(8,128)(2,1)}, bf16[64,256,1,256]{3,1,2,0:T(8,128)(2,1)S(1)}, u32[]{:S(2)}) %copy-start.2) | copy-done | bytes 8388632
  41.1 2.4 %fusion.27 = (f32[64,16]{1,0:T(8,128)S(1)}, f32[64,16,256]{2,1,0:T(8,128)S(1)}) fusion(bf16[64,16,256]{2,1,0:T(8,128)(2,1)S(1)} %bitcast.49, bf16[64,256,1,256]{3,1,2,0:T(8,128)(2,1)S(1)} %get-tuple-element.8, pred[64,256]{1,0:T(8,128)(4,1)S(1)} %get-tuple-element.9), kind=kOutput, calls=%fused_computation.32 | convolution fusion | flops 135003136 | bytes 9981952 | tf_op jit(solution)/shard_map/bkgd,bskd->bkgs/dot_general | solution.py:27
  43.5 13.3 %pmax.7 = f32[64,1,16]{2,0,1:T(8,128)S(1)} all-reduce(f32[64,1,16]{2,0,1:T(8,128)S(1)} %get-tuple-element.5), channel_id=1, replica_groups=mesh['rep'=1,'dp'=2,'sp'=4] {'sp'}, use_global_device_ids=true, to_apply=%region_1.2 | all-reduce | flops 1024 | bytes 8192 | tf_op jit(solution)/shard_map/pmax | solution.py:34
  56.8 0.4 fusion.17
  57.2 0.4 copy.18
  57.6 4.7 %fusion.10 = f32[64,1,16,256]{3,2,0,1:T(8,128)S(1)} fusion(bf16[64,256,1,256]{3,1,2,0:T(8,128)(2,1)} %get-tuple-element.7, f32[64,16,256]{2,1,0:T(8,128)S(1)} %get-tuple-element.12, f32[64,16]{1,0:T(8,128)S(1)} %get-tuple-element.3, f32[64,16]{1,0:T(8,128)S(1)} %get-tuple-element.6), kind=kOutput, calls=%fused_computation.10 | convolution fusion | flops 135004160 | bytes 10493952 | tf_op jit(solution)/shard_map/bkgs,bskd->bkgd/dot_general | solution.py:33
  62.3 1.3 pad_maximum_fusion
  63.6 0.0 all-reduce.3.cloned.1.call-update
  63.6 37.5 %all-reduce.3.cloned.1.call-done = f32[64,1,16,257]{3,2,0,1:T(8,128)} async-done(((f32[64,1,16,257]{3,2,0,1:T(8,128)}), f32[64,1,16,257]{3,2,0,1:T(8,128)}) %all-reduce.3.cloned.1.call-update) | async-done | bytes 1052688 | tf_op jit(solution)/shard_map/psum | solution.py:37
  101.1 1.1 slice.9
  102.2 0.4 copy.23
  102.6 1.4 %fusion.16 = bf16[64,1,16,256]{3,2,0,1:T(8,128)(2,1)S(1)} fusion(f32[64,1,16,257]{3,2,0,1:T(8,128)} %all-reduce.3.cloned.1.call-done, f32[64,16]{1,0:T(8,128)S(1)} %bitcast.52), kind=kLoop, calls=%fused_computation.15 | loop fusion | flops 524288 | bytes 1576960 | tf_op jit(solution)/shard_map/convert_element_type | solution.py:38
  104.1 0.2 copy.25
  104.3 0.0 copy-start.1
  104.3 5.1 %fusion.21 = f32[64,4096]{1,0:T(8,128)S(1)} fusion(bf16[1024,4096]{1,0:T(8,128)(2,1)} %param.13, bf16[64,4096]{1,0:T(8,128)(2,1)S(1)} %bitcast.51, s32[]{:T(128)S(6)} %select_n.18), kind=kOutput, calls=%fused_computation.20 | convolution fusion | flops 536870912 | bytes 9568260 | tf_op jit(solution)/shard_map/dot_general | solution.py:42
  109.4 26.2 %all-reduce.4 = bf16[64,4096]{1,0:T(8,128)(2,1)} all-reduce(f32[64,4096]{1,0:T(8,128)S(1)} %fusion.21), channel_id=1, replica_groups=mesh['rep'=1,'dp'=2,'sp'=4] {'sp'}, use_global_device_ids=true, to_apply=%region_4.5 | all-reduce | flops 262144 | bytes 1572864 | tf_op jit(solution)/shard_map/psum | solution.py:43
  (7 shorter events, 0.0 us)
Async XLA Ops:
  7.2 1.6 %copy-start = (bf16[4096,256]{1,0:T(8,128)(2,1)S(1)}, bf16[4096,256]{1,0:T(8,128)(2,1)}, u32[]{:S(2)}) copy-start(bf16[4096,256]{1,0:T(8,128)(2,1)} %param.11) | copy-start | bytes 6291460
  7.2 93.9 %all-reduce.3.cloned.1.call-start = ((), (), s32[]{:S(2)}) async-start(), calls=%async_computation | async-start | bytes 3145728 | tf_op jit(solution)/shard_map/psum | solution.py:37
  10.3 19.4 %slice-start = ((s8[8388608]{0:T(1024)(128)(4,1)}), s8[4194304]{0:T(1024)(128)(4,1)S(1)}, s32[]{:S(2)}) async-start(s8[8388608]{0:T(1024)(128)(4,1)} %bitcast.46), calls=%async_computation.1 | async-start | bytes 8388608
  12.6 16.9 %copy-start.3 = (s32[64]{0:T(128)S(1)}, s32[64]{0:T(128)}, u32[]{:S(2)}) copy-start(s32[64]{0:T(128)} %param.17) | copy-start | bytes 772
  12.7 16.9 %copy-start.4 = (s32[64]{0:T(128)S(1)}, s32[64]{0:T(128)}, u32[]{:S(2)}) copy-start(s32[64]{0:T(128)} %param.16) | copy-start | bytes 772
  12.7 17.0 %slice-start.1 = ((s8[8388608]{0:T(1024)(128)(4,1)}), s8[4194304]{0:T(1024)(128)(4,1)S(1)}, s32[]{:S(2)}) async-start(s8[8388608]{0:T(1024)(128)(4,1)} %bitcast.46), calls=%async_computation.2 | async-start | bytes 8388608
  37.7 3.4 %copy-start.2 = (bf16[64,256,1,256]{3,1,2,0:T(8,128)(2,1)}, bf16[64,256,1,256]{3,1,2,0:T(8,128)(2,1)S(1)}, u32[]{:S(2)}) copy-start(bf16[64,256,1,256]{3,1,2,0:T(8,128)(2,1)S(1)} %get-tuple-element.8) | copy-start | bytes 25165828
  104.3 31.3 %copy-start.1 = (bf16[4096,256]{1,0:T(8,128)(2,1)S(1)}, bf16[4096,256]{1,0:T(8,128)(2,1)}, u32[]{:S(2)}) copy-start(bf16[4096,256]{1,0:T(8,128)(2,1)} %param.11) | copy-start | bytes 6291460
Sparse Core Ops, SparseCore 0:
  63.8 37.3 all-reduce.2
where the time goes:
time: 143 us; the launch traced here: 142 us
  blocking collectives  39.4 us (28%)
  waiting for transfers between devices  37.5 us (26%)
  matrix products  32.8 us (23%)
  between operations  14.2 us (10%)
  other arithmetic  11.2 us (8%)
  local copies, waits for them, and re-layouts  7.2 us (5%)
    psum x1, waiting for transfers between devices, local_step(): packed = lax.psum(packed, 'sp')  37.5 us
    psum x1, blocking collectives, local_step(): attn_out = lax.psum(partial_out, 'sp').astype(jnp.bfloat16)  26.2 us
    dot_general x1, matrix products, local_step(): jnp.dot(hidden, w_query, preferred_element_type=jnp.float32)  16.8 us
    pmax x1, blocking collectives, local_step(): global_max = lax.pmax(local_max, 'sp')  13.3 us
    select_n x1, other arithmetic, local_step(): jnp.where(at_pos, value_new.reshape(num_rows, 1, kv_heads, head_dim), v_c...  8.02 us
    unnamed x16, local copies, waits for them, and re-layouts  5.24 us
    dot_general x1, matrix products, local_step(): partial_out = jnp.dot(attn_mine, w_out, preferred_element_type=jnp.float32)  5.1 us
    dot_general x1, matrix products, local_step(): jnp.einsum('bkgs,bskd->bkgd', weights.astype(jnp.bfloat16), v_next, prefe...  4.67 us
  transfers between devices with their start and end apart: 1, of which 1 were waited for; matrix products, arithmetic and copies ran while one was open for 0% of the time, Pallas kernels for 0%

commit v1 on v0

v1 whole, which is shorter than its diff:
```python
import jax
import jax.numpy as jnp
from jax import lax
from jax.experimental import pallas as pl
from jax.experimental.pallas import tpu as pltpu
from jax.sharding import PartitionSpec as P

MESH = pl.DeviceIdType.MESH
F32, BF16 = jnp.float32, jnp.bfloat16
LOWEST = float(jnp.finfo(jnp.float32).min)

ROWS = 64
SEQ = 256
DIM = 4096
HD = 256
HEADS = 16
GROUP = 8
CHUNK = 16
NCH = ROWS // CHUNK
NPAIR = CHUNK // 2
CR = NPAIR * 8
HALF = 32
BLK = 1024
NW = 9


def step_kernel(hid_hbm, wq_hbm, wk_hbm, wv_hbm, wo_hbm, kc_hbm, vc_hbm, wp_hbm, vl_hbm,
                out_ref, k_ref, v_ref,
                hid, wbuf, wo, wp, vl, qf, kvn, qsend, qrecv, rowid,
                acc, ml, racc1, rml1, racc2, rml2, osum, obf,
                pd, px, pk, rd, rx, fin,
                s_in, s_w, s_k, s_v, s_wo,
                qs, qr, a1s, a1r, m1s, m1r, a2s, a2r, m2s, m2r,
                rds, rdr, rxs, rxr, gxs, gxr, gds, gdr, grs, grr):
    sp = lax.axis_index('sp')
    x, c = sp // 2, sp % 2
    sib = 2 * x + (1 - c)
    xp = 2 * (1 - x) + c
    first_pos = sp * SEQ

    def remote(src, dst, ss, rs, peer):
        return pltpu.make_async_remote_copy(src_ref=src, dst_ref=dst, send_sem=ss, recv_sem=rs,
                                            device_id={'sp': peer}, device_id_type=MESH)

    hid_cp = pltpu.make_async_copy(hid_hbm, hid, s_in.at[0])
    wp_cp = pltpu.make_async_copy(wp_hbm, wp, s_in.at[1])
    vl_cp = pltpu.make_async_copy(vl_hbm, vl, s_in.at[2])
    hid_cp.start()

    def wq_cp(i):
        cols = pl.ds(pl.multiple_of((8 * c + i) * HD, HD), HD)
        return pltpu.make_async_copy(wq_hbm.at[:, cols], wbuf.at[i], s_w.at[i])

    def k_cp(g):
        rows = pl.ds(g * GROUP * SEQ, GROUP * SEQ)
        return pltpu.make_async_copy(kc_hbm.at[rows], k_ref.at[rows], s_k.at[g])

    def v_cp(g):
        rows = pl.ds(g * GROUP * SEQ, GROUP * SEQ)
        return pltpu.make_async_copy(vc_hbm.at[rows], v_ref.at[rows], s_v.at[g])

    def wo_cp(i):
        rows = pl.ds(i * 256, 256)
        return pltpu.make_async_copy(wo_hbm.at[rows], wo.at[rows], s_wo.at[i])

    def start_w(i, _):
        wq_cp(i).start()
        return 0

    lax.fori_loop(0, 8, start_w, 0)

    @pl.when(c == 0)
    def _():
        pltpu.make_async_copy(wk_hbm, wbuf.at[8], s_w.at[8]).start()

    @pl.when(c == 1)
    def _():
        pltpu.make_async_copy(wv_hbm, wbuf.at[8], s_w.at[8]).start()

    wp_cp.start()
    vl_cp.start()

    barrier = pltpu.get_barrier_semaphore()
    for peer in (sib, xp):
        pl.semaphore_signal(barrier, inc=1, device_id={'sp': peer}, device_id_type=MESH)

    rowid[...] = lax.broadcasted_iota(jnp.int32, (SEQ, HD), 0).astype(F32).astype(BF16)
    hid_cp.wait()
    pl.semaphore_wait(barrier, 2)

    def spread(slot, q):
        for h in range(2):
            qf[h, pl.ds(slot, ROWS, stride=HEADS), :] = q[:, h * 128:(h + 1) * 128]

    def project(i):
        pltpu.make_async_copy(wk_hbm, wbuf.at[i], s_w.at[i]).wait()
        res = jnp.dot(hid[...], wbuf[i], preferred_element_type=F32).astype(BF16)
        qsend[i] = res
        remote(qsend.at[i], qrecv.at[i], qs.at[i], qr.at[i], sib).start()
        return res.astype(F32)

    def head_step(i, _):
        res = project(i)
        slot = 8 * (i // 4) + 4 * c + i % 4
        spread(slot, res)
        k_cp(i).start()
        v_cp(i).start()
        return 0

    lax.fori_loop(0, 8, head_step, 0)
    kvn[c] = project(8)
    for i in range(4):
        wo_cp(i).start()

    def q_desc(i):
        return remote(qsend.at[i], qrecv.at[i], qs.at[i], qr.at[i], sib)

    def take_head(i, _):
        q_desc(i).wait_recv()
        slot = 8 * (i // 4) + 4 * (1 - c) + i % 4
        spread(slot, qrecv[i].astype(F32))
        return 0

    lax.fori_loop(0, 8, take_head, 0)
    q_desc(8).wait_recv()
    kvn[1 - c] = qrecv[8].astype(F32)
    wp_cp.wait()
    vl_cp.wait()

    sub = lax.broadcasted_iota(jnp.int32, (8, HD), 0)
    sub1 = lax.broadcasted_iota(jnp.int32, (8, 128), 0)
    lane1 = lax.broadcasted_iota(jnp.int32, (8, 128), 1)
    lane = lax.broadcasted_iota(jnp.int32, (HEADS, SEQ), 1)

    def insert(ref, b, new):
        rows = pl.ds(pl.multiple_of(b * SEQ, SEQ), SEQ)
        old = ref[rows, :]
        pos = jnp.full((16, HD), (wp[b] - first_pos).astype(F32), F32).astype(BF16)
        row16 = jnp.broadcast_to(new[pl.ds(b, 1), :], (16, HD)).astype(BF16)
        parts = []
        for r in range(SEQ // 16):
            hit = rowid[r * 16:(r + 1) * 16, :] == pos
            parts.append(jnp.where(hit, row16, old[r * 16:(r + 1) * 16, :]))
        both = jnp.concatenate(parts, axis=0)
        ref[rows, :] = both
        return both

    def attend(b):
        kb = insert(k_ref, b, kvn.at[0])
        vb = insert(v_ref, b, kvn.at[1])
        rows = pl.ds(pl.multiple_of(b * HEADS, HEADS), HEADS)
        q = jnp.concatenate([qf[0, rows, :], qf[1, rows, :]], axis=1).astype(BF16)
        s = lax.dot_general(q, kb, (((1,), (1,)), ((), ())), preferred_element_type=F32) * (HD ** -0.5)
        s = jnp.where(lane < vl[b] - first_pos, s, -jnp.inf)
        m = jnp.maximum(jnp.max(s, axis=1, keepdims=True), LOWEST)
        p = jnp.exp(s - m)
        l = jnp.sum(p, axis=1, keepdims=True)
        o = jnp.dot(p.astype(BF16), vb, preferred_element_type=F32)
        return o, jnp.broadcast_to(m, (HEADS, 128)), jnp.broadcast_to(l, (HEADS, 128))

    def pack(t0, t1, low):
        return (jnp.where(low, t0, pltpu.roll(t1, 4, 0)), jnp.where(low, pltpu.roll(t0, 4, 0), t1))

    def chunk_attention(ch):
        def group(g2, tiles):
            g = 2 * ch + g2
            k_cp(g).wait()
            v_cp(g).wait()
            tiles = list(tiles)
            res = [attend(g * GROUP + j) for j in range(GROUP)]
            for jp in range(GROUP // 2):
                (o0, m0, l0), (o1, m1, l1) = res[2 * jp], res[2 * jp + 1]
                p = g2 * (GROUP // 2) + jp
                for core in range(2):
                    r = slice(8 * core, 8 * core + 8)
                    os = pack(o0[r], o1[r], sub < 4)
                    ms = pack(m0[r], m1[r], sub1 < 4)
                    ls = pack(l0[r], l1[r], sub1 < 4)
                    for xd in range(2):
                        acc[core, ch, xd, pl.ds(pl.multiple_of(p * 8, 8), 8), :] = os[xd]
                        t = tiles[2 * core + xd]
                        t = jnp.where(lane1 == p, ms[xd], t)
                        tiles[2 * core + xd] = jnp.where(lane1 == p + 64, ls[xd], t)
            return tuple(tiles)

        zero = jnp.zeros((8, 128), F32)
        tiles = lax.fori_loop(0, 2, group, (zero,) * 4)
        for core in range(2):
            for xd in range(2):
                ml[core, ch, xd] = tiles[2 * core + xd]

    def d2d(ch):
        return (remote(acc.at[1 - c, ch], racc1.at[ch], a1s.at[ch], a1r.at[ch], sib),
                remote(ml.at[1 - c, ch], rml1.at[ch], m1s.at[ch], m1r.at[ch], sib))

    def xlink(ch):
        return (remote(acc.at[c, ch, 1 - x], racc2.at[ch], a2s.at[ch], a2r.at[ch], xp),
                remote(ml.at[c, ch, 1 - x], rml2.at[ch], m2s.at[ch], m2r.at[ch], xp))

    def scales(mla, mlb):
        top = jnp.maximum(mla, mlb)
        sa, sb = jnp.exp(mla - top), jnp.exp(mlb - top)
        total = mla * pltpu.roll(sa, 64, 1) + mlb * pltpu.roll(sb, 64, 1)
        return top, sa, sb, total

    def merge_core(ch):
        for desc in d2d(ch):
            desc.wait_recv()
        for xd in range(2):
            top, sa, sb, total = scales(ml[c, ch, xd], rml1[ch, xd])
            ml[c, ch, xd] = jnp.where(lane1 < 64, top, total)
            for p in range(NPAIR):
                r = slice(p * 8, p * 8 + 8)
                acc[c, ch, xd, r, :] = (acc[c, ch, xd, r, :] * sa[:, p:p + 1]
                                        + racc1[ch, xd, r, :] * sb[:, p:p + 1])
        for desc in xlink(ch):
            desc.start()

    def merge_chip(ch):
        for desc in xlink(ch):
            desc.wait_recv()
        top, sa, sb, total = scales(ml[c, ch, x], rml2[ch])
        inv = pltpu.roll(1.0 / jnp.where(lane1 < 64, 1.0, total), 64, 1)
        sa, sb = sa * inv, sb * inv
        for p in range(NPAIR):
            r = slice(p * 8, p * 8 + 8)
            o = acc[c, ch, x, r, :] * sa[:, p:p + 1] + racc2[ch, r, :] * sb[:, p:p + 1]
            for h in range(2):
                osum[h, pl.ds(pl.multiple_of(ch * CR + p * 8, 8), 8), :] = o[:, h * 128:(h + 1) * 128]

    def core_sum(hf, xd):
        return remote(pd.at[hf, xd], rd.at[hf, xd], rds.at[2 * hf + xd], rdr.at[2 * hf + xd], sib)

    def chip_sum(hf):
        return remote(px.at[hf], rx.at[hf], rxs.at[hf], rxr.at[hf], xp)

    def project_out(hf):
        rows = pl.ds(hf * HALF, HALF)
        for r in range(4):
            for h in range(2):
                lanes = slice(r * HD + h * 128, r * HD + (h + 1) * 128)
                obf[rows, lanes] = osum[h, pl.ds(hf * 4 * HALF + r, HALF, stride=4), :].astype(BF16)

        def block(dst, j):
            def piece(n, _):
                cols = pl.ds(pl.multiple_of(j * BLK + n * 512, 512), 512)
                dst[:, pl.ds(pl.multiple_of(n * 512, 512), 512)] = jnp.dot(
                    obf[rows, :], wo[:, cols], preferred_element_type=F32)
                return 0
            lax.fori_loop(0, BLK // 512, piece, 0)

        block(pd.at[hf, 0], 2 * (1 - x) + 1 - c)
        core_sum(hf, 0).start()
        block(px.at[hf], 2 * (1 - x) + c)
        core_sum(hf, 0).wait_recv()
        px[hf] = px[hf] + rd[hf, 0]
        chip_sum(hf).start()
        block(pd.at[hf, 1], 2 * x + 1 - c)
        core_sum(hf, 1).start()
        block(pk.at[hf], 2 * x + c)

    def own(hf, j):
        return fin.at[j, pl.ds(hf * HALF, HALF)]

    def gather_x(hf):
        return remote(own(hf, sp), own(hf, sp), gxs.at[hf], gxr.at[hf], xp)

    def gather_d(hf):
        return remote(own(hf, sp), own(hf, sp), gds.at[hf], gdr.at[hf], sib)

    def gather_r(hf):
        return remote(own(hf, xp), own(hf, xp), grs.at[hf], grr.at[hf], sib)

    def finish(hf):
        core_sum(hf, 1).wait_recv()
        chip_sum(hf).wait_recv()
        fin[sp, pl.ds(hf * HALF, HALF), :] = ((pk[hf] + rd[hf, 1]) + rx[hf]).astype(BF16)
        gather_x(hf).start()
        gather_d(hf).start()

    def relay(hf):
        remote(own(hf, sp), own(hf, xp), gxs.at[hf], gxr.at[hf], xp).wait_recv()
        gather_r(hf).start()

    def pipeline(ch, _):
        @pl.when(ch < NCH)
        def _():
            chunk_attention(ch)
            for desc in d2d(ch):
                desc.start()

        @pl.when(ch >= 1)
        def _():
            merge_core(ch - 1)
        return 0

    lax.fori_loop(0, NCH + 1, pipeline, 0)

    def chips(ch, _):
        merge_chip(ch)
        return 0

    lax.fori_loop(0, 2, chips, 0)
    for i in range(4):
        wo_cp(i).wait()
    project_out(0)
    lax.fori_loop(2, NCH, chips, 0)
    project_out(1)
    finish(0)
    relay(0)
    finish(1)
    relay(1)

    for hf in range(2):
        gather_d(hf).wait_recv()
        gather_r(hf).wait_recv()
    for j in range(4):
        out_ref[:, j * BLK:(j + 1) * BLK] = fin[j]

    def end_q(i, _):
        q_desc(i).wait_send()
        return 0

    lax.fori_loop(0, NW, end_q, 0)

    def end_chunk(ch, _):
        for desc in d2d(ch) + xlink(ch):
            desc.wait_send()
        return 0

    lax.fori_loop(0, NCH, end_chunk, 0)
    for hf in range(2):
        core_sum(hf, 0).wait_send()
        core_sum(hf, 1).wait_send()
        chip_sum(hf).wait_send()
        gather_x(hf).wait_send()
        gather_d(hf).wait_send()
        gather_r(hf).wait_send()


def solution(mesh):
    row_spec = P(('rep', 'dp'), None)
    cache_spec = P(('rep', 'dp'), 'sp', None, None)
    len_spec = P(('rep', 'dp'))

    def local_step(hidden, w_query, w_key, w_value, w_out, k_cache, v_cache, write_pos, valid_len):
        flat = (ROWS * SEQ, HD)
        args = (hidden, w_query, w_key, w_value, w_out, k_cache.reshape(flat), v_cache.reshape(flat),
                write_pos, valid_len)
        args = tuple(pltpu.with_memory_space_constraint(a, pltpu.HBM) for a in args)
        vm = pl.BlockSpec(memory_space=pltpu.VMEM)
        dma = pltpu.SemaphoreType.DMA
        out, k_new, v_new = pl.pallas_call(
            step_kernel,
            out_shape=[pltpu.VMEM((ROWS, DIM), BF16), pltpu.VMEM(flat, BF16), pltpu.VMEM(flat, BF16)],
            in_specs=[pl.BlockSpec(memory_space=pltpu.HBM)] * 9,
            out_specs=[vm, vm, vm],
            scratch_shapes=[
                pltpu.VMEM((ROWS, DIM), BF16),
                pltpu.VMEM((NW, DIM, HD), BF16),
                pltpu.VMEM((BLK, DIM), BF16),
                pltpu.SMEM((ROWS,), jnp.int32),
                pltpu.SMEM((ROWS,), jnp.int32),
                pltpu.VMEM((2, ROWS * HEADS, 128), F32),
                pltpu.VMEM((2, ROWS, HD), F32),
                pltpu.VMEM((NW, ROWS, HD), BF16),
                pltpu.VMEM((NW, ROWS, HD), BF16),
                pltpu.VMEM((SEQ, HD), BF16),
                pltpu.VMEM((2, NCH, 2, CR, HD), F32),
                pltpu.VMEM((2, NCH, 2, 8, 128), F32),
                pltpu.VMEM((NCH, 2, CR, HD), F32),
                pltpu.VMEM((NCH, 2, 8, 128), F32),
                pltpu.VMEM((NCH, CR, HD), F32),
                pltpu.VMEM((NCH, 8, 128), F32),
                pltpu.VMEM((2, 4 * ROWS, 128), F32),
                pltpu.VMEM((ROWS, BLK), BF16),
                pltpu.VMEM((2, 2, HALF, BLK), F32),
                pltpu.VMEM((2, HALF, BLK), F32),
                pltpu.VMEM((2, HALF, BLK), F32),
                pltpu.VMEM((2, 2, HALF, BLK), F32),
                pltpu.VMEM((2, HALF, BLK), F32),
                pltpu.VMEM((4, ROWS, BLK), BF16),
                dma((3,)), dma((NW,)), dma((8,)), dma((8,)), dma((4,)),
                dma((NW,)), dma((NW,)),
                dma((NCH,)), dma((NCH,)), dma((NCH,)), dma((NCH,)),
                dma((NCH,)), dma((NCH,)), dma((NCH,)), dma((NCH,)),
                dma((4,)), dma((4,)), dma((2,)), dma((2,)),
                dma((2,)), dma((2,)), dma((2,)), dma((2,)), dma((2,)), dma((2,)),
            ],
            compiler_params=pltpu.CompilerParams(
                vmem_limit_bytes=44 * 2 ** 20, collective_id=0, has_side_effects=True),
            name='decode_step',
        )(*args)
        return out, k_new.reshape(k_cache.shape), v_new.reshape(v_cache.shape)

    return jax.shard_map(local_step, mesh=mesh, in_specs=(row_spec, P(), P(), P(), P('sp', None), cache_spec, cache_spec, len_spec, len_spec), out_specs=(row_spec, cache_spec, cache_spec), check_vma=False)
```

time: 143 us -> 56.2 us (0.39)
  Pallas kernels: 0 us -> 47.9 us
  blocking collectives: 39.4 us -> 0 us
  waiting for transfers between devices: 37.5 us -> 0 us
  matrix products: 32.8 us -> 0 us
  between operations: 14.2 us -> 0.64 us
  other arithmetic: 11.2 us -> 0 us
    pallas_call x0 -> x1, Pallas kernels: none -> 47.9 us  [local_step(): pl.pallas_call(step_kernel, out_shape=[pltpu.VMEM((ROWS, DIM), BF16), plt...]
    psum x1 -> x0, waiting for transfers between devices: 37.5 us -> none  [local_step(): packed = lax.psum(packed, 'sp')]
    dot_general x6 -> x0, matrix products: 32.8 us -> none  [the longest x1 16.8 us: local_step(): jnp.dot(hidden, w_query, preferred_element_type=jnp.float32)]
    psum x1 -> x0, blocking collectives: 26.2 us -> none  [local_step(): attn_out = lax.psum(partial_out, 'sp').astype(jnp.bfloat16)]
    pmax x1 -> x0, blocking collectives: 13.3 us -> none  [local_step(): global_max = lax.pmax(local_max, 'sp')]
    select_n x1 -> x0, other arithmetic: 8.02 us -> none  [local_step(): jnp.where(at_pos, value_new.reshape(num_rows, 1, kv_heads, head_dim), v_c...]
    unnamed x16 -> x3, local copies, waits for them, and re-layouts: 5.24 us -> 7.59 us
    convert_element_type x1 -> x0, other arithmetic: 1.45 us -> none  [local_step(): (packed[..., :head_dim] / packed[..., head_dim:]).astype(jnp.bfloat16)]
  transfers between devices with their start and end apart: 1 -> 0, of which waited for: 1 -> 0; matrix products, arithmetic and copies ran while one was open for 0% -> 0% of each run, Pallas kernels for 0% -> 0%
where the time goes in v1:
time: 56.2 us; the launch traced here: 56.1 us
  Pallas kernels  47.9 us (85%)
  local copies, waits for them, and re-layouts  7.59 us (14%)
  between operations  0.64 us (1%)
    pallas_call x1, Pallas kernels, local_step(): pl.pallas_call(step_kernel, out_shape=[pltpu.VMEM((ROWS, DIM), BF16), plt...  47.9 us
    unnamed x3, local copies, waits for them, and re-layouts  7.59 us

profile of v1, /device:TPU:0, one launch (start us, length us, event | category | flops | bytes accessed | tf_op | source)
XLA Modules:
  0.0 56.1 jit_solution(3760566146856864246)
XLA Ops:
  0.6 47.9 %decode_step.1 = (bf16[64,4096]{1,0:T(8,128)(2,1)S(1)}, bf16[16384,256]{1,0:T(8,128)(2,1)S(1)}, bf16[16384,256]{1,0:T(8,128)(2,1)S(1)}) custom-call(bf16[64,4096]{1,0:T(8,128)(2,1)} %hid_hbm.1, bf16[4096,4096]{1,0:T(8,128)(2,1)} %wq_hbm.1, bf16[4096,256]{1,0:T(8,128)(2,1)} %wk_hbm.1, bf16[4096,256]{1,0:T(8,128)(2,1)} %wv_hbm.1, bf16[1024,4096]{1,0:T(8,128)(2,1)} %wo_hbm.1, ...), custom_call_target="tpu_custom_call" | custom-call | tf_op jit(solution)/shard_map/decode_step/pallas_call | solution.py:353
  48.5 0.8 %copy.17 = bf16[64,4096]{1,0:T(8,128)(2,1)} copy(bf16[64,4096]{1,0:T(8,128)(2,1)S(1)} %get-tuple-element.12) | data formatting | bytes 1048576
  49.3 3.4 %copy.18 = bf16[64,256,1,256]{3,1,2,0:T(8,128)(2,1)} copy(bf16[64,256,1,256]{3,1,2,0:T(8,128)(2,1)S(1)} %bitcast.9) | data formatting | bytes 16777216
  52.7 3.4 %copy.19 = bf16[64,256,1,256]{3,1,2,0:T(8,128)(2,1)} copy(bf16[64,256,1,256]{3,1,2,0:T(8,128)(2,1)S(1)} %bitcast.8) | data formatting | bytes 16777216

commit v2 on v1

--- a/solution.py
+++ b/solution.py
@@ -25,8 +25,8 @@
 
 
 def step_kernel(hid_hbm, wq_hbm, wk_hbm, wv_hbm, wo_hbm, kc_hbm, vc_hbm, wp_hbm, vl_hbm,
-                out_ref, k_ref, v_ref,
-                hid, wbuf, wo, wp, vl, qf, kvn, qsend, qrecv, rowid,
+                out_ref, k_ref, v_ref, kvn,
+                hid, wbuf, wo, wp, vl, qf, qsend, qrecv, prob, pnew,
                 acc, ml, racc1, rml1, racc2, rml2, osum, obf,
                 pd, px, pk, rd, rx, fin,
                 s_in, s_w, s_k, s_v, s_wo,
@@ -84,7 +84,6 @@
     for peer in (sib, xp):
         pl.semaphore_signal(barrier, inc=1, device_id={'sp': peer}, device_id_type=MESH)
 
-    rowid[...] = lax.broadcasted_iota(jnp.int32, (SEQ, HD), 0).astype(F32).astype(BF16)
     hid_cp.wait()
     pl.semaphore_wait(barrier, 2)
 
@@ -132,62 +131,70 @@
     lane1 = lax.broadcasted_iota(jnp.int32, (8, 128), 1)
     lane = lax.broadcasted_iota(jnp.int32, (HEADS, SEQ), 1)
 
-    def insert(ref, b, new):
-        rows = pl.ds(pl.multiple_of(b * SEQ, SEQ), SEQ)
-        old = ref[rows, :]
-        pos = jnp.full((16, HD), (wp[b] - first_pos).astype(F32), F32).astype(BF16)
-        row16 = jnp.broadcast_to(new[pl.ds(b, 1), :], (16, HD)).astype(BF16)
-        parts = []
-        for r in range(SEQ // 16):
-            hit = rowid[r * 16:(r + 1) * 16, :] == pos
-            parts.append(jnp.where(hit, row16, old[r * 16:(r + 1) * 16, :]))
-        both = jnp.concatenate(parts, axis=0)
-        ref[rows, :] = both
-        return both
-
-    def attend(b):
-        kb = insert(k_ref, b, kvn.at[0])
-        vb = insert(v_ref, b, kvn.at[1])
+    def cache_rows(b):
+        return pl.ds(pl.multiple_of(b * SEQ, SEQ), SEQ)
+
+    def weigh(b, j):
         rows = pl.ds(pl.multiple_of(b * HEADS, HEADS), HEADS)
-        q = jnp.concatenate([qf[0, rows, :], qf[1, rows, :]], axis=1).astype(BF16)
-        s = lax.dot_general(q, kb, (((1,), (1,)), ((), ())), preferred_element_type=F32) * (HD ** -0.5)
+        q = jnp.concatenate([qf[0, rows, :], qf[1, rows, :]], axis=1)
+        s = lax.dot_general(q.astype(BF16), k_ref[cache_rows(b), :], (((1,), (1,)), ((), ())),
+                            preferred_element_type=F32)
+        s_new = jnp.sum(q * kvn[0, pl.ds(b, 1), :], axis=1, keepdims=True)
+        here = lane == wp[b] - first_pos
+        s = jnp.where(here, s_new, s) * (HD ** -0.5)
         s = jnp.where(lane < vl[b] - first_pos, s, -jnp.inf)
         m = jnp.maximum(jnp.max(s, axis=1, keepdims=True), LOWEST)
         p = jnp.exp(s - m)
         l = jnp.sum(p, axis=1, keepdims=True)
-        o = jnp.dot(p.astype(BF16), vb, preferred_element_type=F32)
-        return o, jnp.broadcast_to(m, (HEADS, 128)), jnp.broadcast_to(l, (HEADS, 128))
+        p_new = jnp.sum(jnp.where(here, p, 0.0), axis=1, keepdims=True)
+        mine = slice(j * HEADS, (j + 1) * HEADS)
+        prob[mine, :] = jnp.where(here, 0.0, p).astype(BF16)
+        pnew[mine, :] = jnp.broadcast_to(p_new, (HEADS, 128))
+        return jnp.broadcast_to(m, (HEADS, 128)), jnp.broadcast_to(l, (HEADS, 128))
+
+    def value_sum(b, j):
+        mine = slice(j * HEADS, (j + 1) * HEADS)
+        o = jnp.dot(prob[mine, :], v_ref[cache_rows(b), :], preferred_element_type=F32)
+        p_new = pnew[mine, :]
+        return o + jnp.concatenate([p_new, p_new], axis=1) * kvn[1, pl.ds(b, 1), :]
 
     def pack(t0, t1, low):
         return (jnp.where(low, t0, pltpu.roll(t1, 4, 0)), jnp.where(low, pltpu.roll(t0, 4, 0), t1))
 
     def chunk_attention(ch):
-        def group(g2, tiles):
-            g = 2 * ch + g2
-            k_cp(g).wait()
-            v_cp(g).wait()
-            tiles = list(tiles)
-            res = [attend(g * GROUP + j) for j in range(GROUP)]
-            for jp in range(GROUP // 2):
-                (o0, m0, l0), (o1, m1, l1) = res[2 * jp], res[2 * jp + 1]
-                p = g2 * (GROUP // 2) + jp
+        for g2 in range(CHUNK // GROUP):
+            k_cp(ch * (CHUNK // GROUP) + g2).wait()
+
+        @pl.when(ch >= 0)
+        def _():
+            tiles = [jnp.zeros((8, 128), F32)] * 4
+            for p in range(NPAIR):
+                m0, l0 = weigh(ch * CHUNK + 2 * p, 2 * p)
+                m1, l1 = weigh(ch * CHUNK + 2 * p + 1, 2 * p + 1)
+                for core in range(2):
+                    r = slice(8 * core, 8 * core + 8)
+                    ms = pack(m0[r], m1[r], sub1 < 4)
+                    ls = pack(l0[r], l1[r], sub1 < 4)
+                    for xd in range(2):
+                        t = jnp.where(lane1 == p, ms[xd], tiles[2 * core + xd])
+                        tiles[2 * core + xd] = jnp.where(lane1 == p + 64, ls[xd], t)
+            for core in range(2):
+                for xd in range(2):
+                    ml[core, ch, xd] = tiles[2 * core + xd]
+
+        for g2 in range(CHUNK // GROUP):
+            v_cp(ch * (CHUNK // GROUP) + g2).wait()
+
+        @pl.when(ch >= 0)
+        def _():
+            for p in range(NPAIR):
+                o0 = value_sum(ch * CHUNK + 2 * p, 2 * p)
+                o1 = value_sum(ch * CHUNK + 2 * p + 1, 2 * p + 1)
                 for core in range(2):
                     r = slice(8 * core, 8 * core + 8)
                     os = pack(o0[r], o1[r], sub < 4)
-                    ms = pack(m0[r], m1[r], sub1 < 4)
-                    ls = pack(l0[r], l1[r], sub1 < 4)
                     for xd in range(2):
-                        acc[core, ch, xd, pl.ds(pl.multiple_of(p * 8, 8), 8), :] = os[xd]
-                        t = tiles[2 * core + xd]
-                        t = jnp.where(lane1 == p, ms[xd], t)
-                        tiles[2 * core + xd] = jnp.where(lane1 == p + 64, ls[xd], t)
-            return tuple(tiles)
-
-        zero = jnp.zeros((8, 128), F32)
-        tiles = lax.fori_loop(0, 2, group, (zero,) * 4)
-        for core in range(2):
-            for xd in range(2):
-                ml[core, ch, xd] = tiles[2 * core + xd]
+                        acc[core, ch, xd, p * 8:p * 8 + 8, :] = os[xd]
 
     def d2d(ch):
         return (remote(acc.at[1 - c, ch], racc1.at[ch], a1s.at[ch], a1r.at[ch], sib),
@@ -338,6 +345,34 @@
         gather_r(hf).wait_send()
 
 
+def cache_kernel(wp, kvn, k_in, v_in, k_ref, v_ref, k_out, v_out, s_k, s_v):
+    first_pos = lax.axis_index('sp') * SEQ
+    row = lax.broadcasted_iota(jnp.int32, (16, HD), 0)
+
+    def insert(b, _):
+        pos = wp[b] - first_pos
+        base = jnp.clip(pos, 0, SEQ - 1) // 16 * 16
+        rows = pl.ds(pl.multiple_of(b * SEQ + base, 16), 16)
+        hit = row == pos - base
+        for ref, i in ((k_ref, 0), (v_ref, 1)):
+            ref[rows, :] = jnp.where(hit, kvn[i, pl.ds(b, 1), :], ref[rows, :].astype(F32)).astype(BF16)
+        return 0
+
+    lax.fori_loop(0, ROWS, insert, 0, unroll=8)
+
+    def copies(g):
+        rows = pl.ds(g * GROUP * SEQ, GROUP * SEQ)
+        return (pltpu.make_async_copy(k_ref.at[rows], k_out.at[rows], s_k.at[g]),
+                pltpu.make_async_copy(v_ref.at[rows], v_out.at[rows], s_v.at[g]))
+
+    for g in range(8):
+        for cp in copies(g):
+            cp.start()
+    for g in range(8):
+        for cp in copies(g):
+            cp.wait()
+
+
 def solution(mesh):
     row_spec = P(('rep', 'dp'), None)
     cache_spec = P(('rep', 'dp'), 'sp', None, None)
@@ -350,11 +385,12 @@
         args = tuple(pltpu.with_memory_space_constraint(a, pltpu.HBM) for a in args)
         vm = pl.BlockSpec(memory_space=pltpu.VMEM)
         dma = pltpu.SemaphoreType.DMA
-        out, k_new, v_new = pl.pallas_call(
+        out, k_old, v_old, kv_new = pl.pallas_call(
             step_kernel,
-            out_shape=[pltpu.VMEM((ROWS, DIM), BF16), pltpu.VMEM(flat, BF16), pltpu.VMEM(flat, BF16)],
+            out_shape=[pltpu.VMEM((ROWS, DIM), BF16), pltpu.VMEM(flat, BF16), pltpu.VMEM(flat, BF16),
+                       pltpu.VMEM((2, ROWS, HD), F32)],
             in_specs=[pl.BlockSpec(memory_space=pltpu.HBM)] * 9,
-            out_specs=[vm, vm, vm],
+            out_specs=[vm, vm, vm, vm],
             scratch_shapes=[
                 pltpu.VMEM((ROWS, DIM), BF16),
                 pltpu.VMEM((NW, DIM, HD), BF16),
@@ -362,10 +398,10 @@
                 pltpu.SMEM((ROWS,), jnp.int32),
                 pltpu.SMEM((ROWS,), jnp.int32),
                 pltpu.VMEM((2, ROWS * HEADS, 128), F32),
-                pltpu.VMEM((2, ROWS, HD), F32),
                 pltpu.VMEM((NW, ROWS, HD), BF16),
                 pltpu.VMEM((NW, ROWS, HD), BF16),
-                pltpu.VMEM((SEQ, HD), BF16),
+                pltpu.VMEM((CHUNK * HEADS, SEQ), BF16),
+                pltpu.VMEM((CHUNK * HEADS, 128), F32),
                 pltpu.VMEM((2, NCH, 2, CR, HD), F32),
                 pltpu.VMEM((2, NCH, 2, 8, 128), F32),
                 pltpu.VMEM((NCH, 2, CR, HD), F32),
@@ -391,6 +427,18 @@
                 vmem_limit_bytes=44 * 2 ** 20, collective_id=0, has_side_effects=True),
             name='decode_step',
         )(*args)
+        anywhere = pl.BlockSpec(memory_space=pltpu.HBM)
+        _, _, k_new, v_new = pl.pallas_call(
+            cache_kernel,
+            out_shape=[pltpu.VMEM(flat, BF16), pltpu.VMEM(flat, BF16),
+                       pltpu.HBM(flat, BF16), pltpu.HBM(flat, BF16)],
+            in_specs=[pl.BlockSpec(memory_space=pltpu.SMEM), vm, vm, vm],
+            out_specs=[vm, vm, anywhere, anywhere],
+            scratch_shapes=[dma((8,)), dma((8,))],
+            input_output_aliases={2: 0, 3: 1},
+            compiler_params=pltpu.CompilerParams(vmem_limit_bytes=2 ** 20),
+            name='cache_update',
+        )(write_pos, kv_new, k_old, v_old)
         return out, k_new.reshape(k_cache.shape), v_new.reshape(v_cache.shape)
 
     return jax.shard_map(local_step, mesh=mesh, in_specs=(row_spec, P(), P(), P(), P('sp', None), cache_spec, cache_spec, len_spec, len_spec), out_specs=(row_spec, cache_spec, cache_spec), check_vma=False)

time: 56.2 us -> 43.4 us (0.77)
  local copies, waits for them, and re-layouts: 7.59 us -> 0.8 us
  Pallas kernels: 47.9 us -> 41.8 us
    pallas_call x1, Pallas kernels: 47.9 us -> 34.8 us  [local_step(): pl.pallas_call(step_kernel, out_shape=[pltpu.VMEM((ROWS, DIM), BF16), plt...]
    pallas_call x0 -> x1, Pallas kernels: none -> 7.08 us  [local_step(): pl.pallas_call(cache_kernel, out_shape=[pltpu.VMEM(flat, BF16), pltpu.VME...]
    unnamed x3, local copies, waits for them, and re-layouts: 7.59 us -> 0.8 us
where the time goes in v2:
time: 43.4 us; the launch traced here: 43.3 us
  Pallas kernels  41.8 us (96%)
  local copies, waits for them, and re-layouts  0.8 us (2%)
  between operations  0.65 us (1%)
    pallas_call x1, Pallas kernels, local_step(): pl.pallas_call(step_kernel, out_shape=[pltpu.VMEM((ROWS, DIM), BF16), plt...  34.8 us
    pallas_call x1, Pallas kernels, local_step(): pl.pallas_call(cache_kernel, out_shape=[pltpu.VMEM(flat, BF16), pltpu.VME...  7.08 us

profile of v2, /device:TPU:0, one launch (start us, length us, event | category | flops | bytes accessed | tf_op | source)
XLA Modules:
  0.0 43.3 jit_solution(16639957978808914490)
XLA Ops:
  0.6 0.0 copy-start
  0.6 34.8 %decode_step.1 = (bf16[64,4096]{1,0:T(8,128)(2,1)S(1)}, bf16[16384,256]{1,0:T(8,128)(2,1)S(1)}, bf16[16384,256]{1,0:T(8,128)(2,1)S(1)}, f32[2,64,256]{2,1,0:T(8,128)S(1)}) custom-call(bf16[64,4096]{1,0:T(8,128)(2,1)} %hid_hbm.1, bf16[4096,4096]{1,0:T(8,128)(2,1)} %wq_hbm.1, bf16[4096,256]{1,0:T(8,128)(2,1)} %wk_hbm.1, bf16[4096,256]{1,0:T(8,128)(2,1)} %wv_hbm.1, ...), custom_call_target="tpu_custom_call" | custom-call | tf_op jit(solution)/shard_map/decode_step/pallas_call | solution.py:388
  35.4 0.8 %copy.19 = bf16[64,4096]{1,0:T(8,128)(2,1)} copy(bf16[64,4096]{1,0:T(8,128)(2,1)S(1)} %get-tuple-element.18) | data formatting | bytes 1048576
  36.2 0.0 copy-done
  36.2 7.1 %cache_update.1 = (bf16[16384,256]{1,0:T(8,128)(2,1)S(1)}, bf16[16384,256]{1,0:T(8,128)(2,1)S(1)}, bf16[16384,256]{1,0:T(8,128)(2,1)}, bf16[16384,256]{1,0:T(8,128)(2,1)}) custom-call(s32[64]{0:T(128)S(1)} %copy-done, f32[2,64,256]{2,1,0:T(8,128)S(1)} %get-tuple-element.10.kvn, ...), custom_call_target="tpu_custom_call", output_to_operand_aliasing={{0}: (2, {}), {1}: (3, {})} | custom-call | tf_op jit(solution)/shard_map/cache_update/pallas_call | solution.py:431
Async XLA Ops:
  0.6 35.6 %copy-start = (s32[64]{0:T(128)S(1)}, s32[64]{0:T(128)}, u32[]{:S(2)}) copy-start(s32[64]{0:T(128)} %wp.1) | copy-start | bytes 772

commit v3 on v2

--- a/solution.py
+++ b/solution.py
@@ -19,19 +19,24 @@
 NCH = ROWS // CHUNK
 NPAIR = CHUNK // 2
 CR = NPAIR * 8
-HALF = 32
+OUT = 16
+NOUT = ROWS // OUT
 BLK = 1024
-NW = 9
+AHEAD = 4
+SHARED = 2
+NOWN = 8 - SHARED
+NW = NOWN + 1
+DIST = 1
 
 
 def step_kernel(hid_hbm, wq_hbm, wk_hbm, wv_hbm, wo_hbm, kc_hbm, vc_hbm, wp_hbm, vl_hbm,
                 out_ref, k_ref, v_ref, kvn,
-                hid, wbuf, wo, wp, vl, qf, qsend, qrecv, prob, pnew,
+                hid, wbuf, wo, wp, vl, qf, qsend, qrecv, qchip, prob, pnew,
                 acc, ml, racc1, rml1, racc2, rml2, osum, obf,
-                pd, px, pk, rd, rx, fin,
+                pd, px, pk, rd, rx,
                 s_in, s_w, s_k, s_v, s_wo,
-                qs, qr, a1s, a1r, m1s, m1r, a2s, a2r, m2s, m2r,
-                rds, rdr, rxs, rxr, gxs, gxr, gds, gdr, grs, grr):
+                qs, qr, qxs, qxr, a1s, a1r, m1s, m1r, a2s, a2r, m2s, m2r,
+                rds, rdr, rxs, rxr):
     sp = lax.axis_index('sp')
     x, c = sp // 2, sp % 2
     sib = 2 * x + (1 - c)
@@ -47,8 +52,11 @@
     vl_cp = pltpu.make_async_copy(vl_hbm, vl, s_in.at[2])
     hid_cp.start()
 
+    def head(i, chip):
+        return i + chip * (7 - 2 * i)
+
     def wq_cp(i):
-        cols = pl.ds(pl.multiple_of((8 * c + i) * HD, HD), HD)
+        cols = pl.ds(pl.multiple_of((8 * c + head(i, x)) * HD, HD), HD)
         return pltpu.make_async_copy(wq_hbm.at[:, cols], wbuf.at[i], s_w.at[i])
 
     def k_cp(g):
@@ -63,20 +71,26 @@
         rows = pl.ds(i * 256, 256)
         return pltpu.make_async_copy(wo_hbm.at[rows], wo.at[rows], s_wo.at[i])
 
-    def start_w(i, _):
+    def start_w(i):
+        @pl.when(i < NOWN)
+        def _():
+            wq_cp(i).start()
+
+        @pl.when((i == NOWN) & (c == 0))
+        def _():
+            pltpu.make_async_copy(wk_hbm, wbuf.at[NOWN], s_w.at[NOWN]).start()
+
+        @pl.when((i == NOWN) & (c == 1))
+        def _():
+            pltpu.make_async_copy(wv_hbm, wbuf.at[NOWN], s_w.at[NOWN]).start()
+
+        @pl.when(i > NOWN)
+        def _():
+            k_cp(i - NW).start()
+            v_cp(i - NW).start()
+
+    for i in range(AHEAD):
         wq_cp(i).start()
-        return 0
-
-    lax.fori_loop(0, 8, start_w, 0)
-
-    @pl.when(c == 0)
-    def _():
-        pltpu.make_async_copy(wk_hbm, wbuf.at[8], s_w.at[8]).start()
-
-    @pl.when(c == 1)
-    def _():
-        pltpu.make_async_copy(wv_hbm, wbuf.at[8], s_w.at[8]).start()
-
     wp_cp.start()
     vl_cp.start()
 
@@ -91,38 +105,59 @@
         for h in range(2):
             qf[h, pl.ds(slot, ROWS, stride=HEADS), :] = q[:, h * 128:(h + 1) * 128]
 
+    def slot(i, chip, core):
+        h = head(i, chip)
+        return 8 * (h // 4) + 4 * core + h % 4
+
+    def q_core(i):
+        return remote(qsend.at[i], qrecv.at[i], qs.at[i], qr.at[i], sib)
+
+    def q_chip(i):
+        return remote(qsend.at[i], qchip.at[i], qxs.at[i], qxr.at[i], xp)
+
+    def q_relay(i):
+        return remote(qchip.at[i], qrecv.at[NW + i], qs.at[NW + i], qr.at[NW + i], sib)
+
     def project(i):
         pltpu.make_async_copy(wk_hbm, wbuf.at[i], s_w.at[i]).wait()
+        start_w(i + AHEAD)
         res = jnp.dot(hid[...], wbuf[i], preferred_element_type=F32).astype(BF16)
         qsend[i] = res
-        remote(qsend.at[i], qrecv.at[i], qs.at[i], qr.at[i], sib).start()
+        q_core(i).start()
         return res.astype(F32)
 
     def head_step(i, _):
         res = project(i)
-        slot = 8 * (i // 4) + 4 * c + i % 4
-        spread(slot, res)
-        k_cp(i).start()
-        v_cp(i).start()
-        return 0
-
-    lax.fori_loop(0, 8, head_step, 0)
-    kvn[c] = project(8)
-    for i in range(4):
-        wo_cp(i).start()
-
-    def q_desc(i):
-        return remote(qsend.at[i], qrecv.at[i], qs.at[i], qr.at[i], sib)
+
+        @pl.when(i < SHARED)
+        def _():
+            q_chip(i).start()
+
+        spread(slot(i, x, c), res)
+        return 0
+
+    lax.fori_loop(0, NOWN, head_step, 0)
+    for i in range(SHARED):
+        q_chip(i).wait_recv()
+        q_relay(i).start()
+    kvn[c] = project(NOWN)
+    for g in range(AHEAD, 8):
+        k_cp(g).start()
+        v_cp(g).start()
+    for i in range(SHARED):
+        spread(slot(i, 1 - x, c), qchip[i].astype(F32))
 
     def take_head(i, _):
-        q_desc(i).wait_recv()
-        slot = 8 * (i // 4) + 4 * (1 - c) + i % 4
-        spread(slot, qrecv[i].astype(F32))
-        return 0
-
-    lax.fori_loop(0, 8, take_head, 0)
-    q_desc(8).wait_recv()
-    kvn[1 - c] = qrecv[8].astype(F32)
+        q_core(i).wait_recv()
+        spread(slot(i, x, 1 - c), qrecv[i].astype(F32))
+        return 0
+
+    lax.fori_loop(0, NOWN, take_head, 0)
+    for i in range(SHARED):
+        q_relay(i).wait_recv()
+        spread(slot(i, 1 - x, 1 - c), qrecv[NW + i].astype(F32))
+    q_core(NOWN).wait_recv()
+    kvn[1 - c] = qrecv[NOWN].astype(F32)
     wp_cp.wait()
     vl_cp.wait()
 
@@ -161,7 +196,7 @@
     def pack(t0, t1, low):
         return (jnp.where(low, t0, pltpu.roll(t1, 4, 0)), jnp.where(low, pltpu.roll(t0, 4, 0), t1))
 
-    def chunk_attention(ch):
+    def chunk_attention(ch, between):
         for g2 in range(CHUNK // GROUP):
             k_cp(ch * (CHUNK // GROUP) + g2).wait()
 
@@ -235,100 +270,94 @@
             for h in range(2):
                 osum[h, pl.ds(pl.multiple_of(ch * CR + p * 8, 8), 8), :] = o[:, h * 128:(h + 1) * 128]
 
-    def core_sum(hf, xd):
-        return remote(pd.at[hf, xd], rd.at[hf, xd], rds.at[2 * hf + xd], rdr.at[2 * hf + xd], sib)
-
-    def chip_sum(hf):
-        return remote(px.at[hf], rx.at[hf], rxs.at[hf], rxr.at[hf], xp)
-
-    def project_out(hf):
-        rows = pl.ds(hf * HALF, HALF)
+    def core_sum(t, xd):
+        return remote(pd.at[t, xd], rd.at[t, xd], rds.at[2 * t + xd], rdr.at[2 * t + xd], sib)
+
+    def chip_sum(t):
+        return remote(px.at[t], rx.at[t], rxs.at[t], rxr.at[t], xp)
+
+    def project_block(dst, t, j):
+        rows = pl.ds(pl.multiple_of(t * OUT, OUT), OUT)
+        cols = pl.ds(pl.multiple_of(j * BLK, BLK), BLK)
+        dst[...] = jnp.dot(obf[rows, :], wo[:, cols], preferred_element_type=F32)
+
+    def project_far(t):
+        rows = pl.ds(pl.multiple_of(t * OUT, OUT), OUT)
         for r in range(4):
             for h in range(2):
                 lanes = slice(r * HD + h * 128, r * HD + (h + 1) * 128)
-                obf[rows, lanes] = osum[h, pl.ds(hf * 4 * HALF + r, HALF, stride=4), :].astype(BF16)
-
-        def block(dst, j):
-            def piece(n, _):
-                cols = pl.ds(pl.multiple_of(j * BLK + n * 512, 512), 512)
-                dst[:, pl.ds(pl.multiple_of(n * 512, 512), 512)] = jnp.dot(
-                    obf[rows, :], wo[:, cols], preferred_element_type=F32)
-                return 0
-            lax.fori_loop(0, BLK // 512, piece, 0)
-
-        block(pd.at[hf, 0], 2 * (1 - x) + 1 - c)
-        core_sum(hf, 0).start()
-        block(px.at[hf], 2 * (1 - x) + c)
-        core_sum(hf, 0).wait_recv()
-        px[hf] = px[hf] + rd[hf, 0]
-        chip_sum(hf).start()
-        block(pd.at[hf, 1], 2 * x + 1 - c)
-        core_sum(hf, 1).start()
-        block(pk.at[hf], 2 * x + c)
-
-    def own(hf, j):
-        return fin.at[j, pl.ds(hf * HALF, HALF)]
-
-    def gather_x(hf):
-        return remote(own(hf, sp), own(hf, sp), gxs.at[hf], gxr.at[hf], xp)
-
-    def gather_d(hf):
-        return remote(own(hf, sp), own(hf, sp), gds.at[hf], gdr.at[hf], sib)
-
-    def gather_r(hf):
-        return remote(own(hf, xp), own(hf, xp), grs.at[hf], grr.at[hf], sib)
-
-    def finish(hf):
-        core_sum(hf, 1).wait_recv()
-        chip_sum(hf).wait_recv()
-        fin[sp, pl.ds(hf * HALF, HALF), :] = ((pk[hf] + rd[hf, 1]) + rx[hf]).astype(BF16)
-        gather_x(hf).start()
-        gather_d(hf).start()
-
-    def relay(hf):
-        remote(own(hf, sp), own(hf, xp), gxs.at[hf], gxr.at[hf], xp).wait_recv()
-        gather_r(hf).start()
+                obf[rows, lanes] = osum[h, pl.ds(t * 4 * OUT + r, OUT, stride=4), :].astype(BF16)
+        project_block(pd.at[t, 0], t, 2 * (1 - x) + 1 - c)
+        project_block(px.at[t], t, 2 * (1 - x) + c)
+        core_sum(t, 0).start()
+
+    def project_near(t):
+        project_block(pd.at[t, 1], t, 2 * x + 1 - c)
+        project_block(pk.at[t], t, 2 * x + c)
+        core_sum(t, 1).start()
+
+    def send_far(t):
+        core_sum(t, 0).wait_recv()
+        px[t] = px[t] + rd[t, 0]
+        chip_sum(t).start()
+
+    def finish(t):
+        core_sum(t, 1).wait_recv()
+        chip_sum(t).wait_recv()
+        out_ref[pl.ds(pl.multiple_of(t * OUT, OUT), OUT), :] = ((pk[t] + rd[t, 1]) + rx[t]).astype(BF16)
 
     def pipeline(ch, _):
-        @pl.when(ch < NCH)
-        def _():
-            chunk_attention(ch)
-            for desc in d2d(ch):
-                desc.start()
-
-        @pl.when(ch >= 1)
-        def _():
-            merge_core(ch - 1)
-        return 0
-
-    lax.fori_loop(0, NCH + 1, pipeline, 0)
-
-    def chips(ch, _):
-        merge_chip(ch)
-        return 0
-
-    lax.fori_loop(0, 2, chips, 0)
+        def earlier():
+            @pl.when(ch >= DIST)
+            def _():
+                merge_core(ch - DIST)
+
+        @pl.when(ch < 4)
+        def _():
+            wo_cp(ch).start()
+
+        chunk_attention(ch, earlier)
+        for desc in d2d(ch):
+            desc.start()
+        earlier()
+        return 0
+
+    lax.fori_loop(0, NCH, pipeline, 0)
+
     for i in range(4):
         wo_cp(i).wait()
-    project_out(0)
-    lax.fori_loop(2, NCH, chips, 0)
-    project_out(1)
-    finish(0)
-    relay(0)
-    finish(1)
-    relay(1)
-
-    for hf in range(2):
-        gather_d(hf).wait_recv()
-        gather_r(hf).wait_recv()
-    for j in range(4):
-        out_ref[:, j * BLK:(j + 1) * BLK] = fin[j]
+
+    def outputs(t, _):
+        for u in range(OUT // CHUNK):
+            merge_chip(t * (OUT // CHUNK) + u)
+        project_far(t)
+
+        @pl.when(t == NOUT - 1)
+        def _():
+            send_far(t - 1)
+
+        project_near(t)
+
+        @pl.when(t == 0)
+        def _():
+            merge_core(NCH - 1)
+
+        @pl.when((t > 0) & (t < NOUT - 1))
+        def _():
+            send_far(t - 1)
+        return 0
+
+    lax.fori_loop(0, NOUT, outputs, 0)
+    send_far(NOUT - 1)
 
     def end_q(i, _):
-        q_desc(i).wait_send()
+        q_core(i).wait_send()
         return 0
 
     lax.fori_loop(0, NW, end_q, 0)
+    for i in range(SHARED):
+        q_chip(i).wait_send()
+        q_relay(i).wait_send()
 
     def end_chunk(ch, _):
         for desc in d2d(ch) + xlink(ch):
@@ -336,41 +365,64 @@
         return 0
 
     lax.fori_loop(0, NCH, end_chunk, 0)
-    for hf in range(2):
-        core_sum(hf, 0).wait_send()
-        core_sum(hf, 1).wait_send()
-        chip_sum(hf).wait_send()
-        gather_x(hf).wait_send()
-        gather_d(hf).wait_send()
-        gather_r(hf).wait_send()
+
+    def end_out(t, _):
+        core_sum(t, 0).wait_send()
+        core_sum(t, 1).wait_send()
+        return 0
+
+    lax.fori_loop(0, NOUT, end_out, 0)
+
+    def finals(t, _):
+        finish(t)
+        chip_sum(t).wait_send()
+        return 0
+
+    lax.fori_loop(0, NOUT, finals, 0)
 
 
 def cache_kernel(wp, kvn, k_in, v_in, k_ref, v_ref, k_out, v_out, s_k, s_v):
     first_pos = lax.axis_index('sp') * SEQ
     row = lax.broadcasted_iota(jnp.int32, (16, HD), 0)
 
-    def insert(b, _):
-        pos = wp[b] - first_pos
-        base = jnp.clip(pos, 0, SEQ - 1) // 16 * 16
-        rows = pl.ds(pl.multiple_of(b * SEQ + base, 16), 16)
-        hit = row == pos - base
-        for ref, i in ((k_ref, 0), (v_ref, 1)):
-            ref[rows, :] = jnp.where(hit, kvn[i, pl.ds(b, 1), :], ref[rows, :].astype(F32)).astype(BF16)
-        return 0
-
-    lax.fori_loop(0, ROWS, insert, 0, unroll=8)
+    def insert(g):
+        for j in range(GROUP):
+            b = g * GROUP + j
+            pos = wp[b] - first_pos
+            base = jnp.clip(pos, 0, SEQ - 1) // 16 * 16
+            rows = pl.ds(pl.multiple_of(b * SEQ + base, 16), 16)
+            hit = row == pos - base
+            for ref, i in ((k_ref, 0), (v_ref, 1)):
+                ref[rows, :] = jnp.where(hit, kvn[i, pl.ds(b, 1), :], ref[rows, :].astype(F32)).astype(BF16)
 
     def copies(g):
         rows = pl.ds(g * GROUP * SEQ, GROUP * SEQ)
         return (pltpu.make_async_copy(k_ref.at[rows], k_out.at[rows], s_k.at[g]),
                 pltpu.make_async_copy(v_ref.at[rows], v_out.at[rows], s_v.at[g]))
 
-    for g in range(8):
-        for cp in copies(g):
-            cp.start()
+    for g in range(9):
+        if g < 8:
+            insert(g)
+        if g >= 1:
+            for cp in copies(g - 1):
+                cp.start()
     for g in range(8):
         for cp in copies(g):
             cp.wait()
+
+
+def join_kernel(b0, b1, b2, b3, out, sems):
+    sp = lax.axis_index('sp')
+    x, c = sp // 2, sp % 2
+    copies = []
+    for i, ref in enumerate((b0, b1, b2, b3)):
+        j = 2 * (x if i < 2 else 1 - x) + (c if i % 2 == 0 else 1 - c)
+        cols = pl.ds(pl.multiple_of(j * BLK, BLK), BLK)
+        copies.append(pltpu.make_async_copy(ref, out.at[:, cols], sems.at[i]))
+    for cp in copies:
+        cp.start()
+    for cp in copies:
+        cp.wait()
 
 
 def solution(mesh):
@@ -387,7 +439,7 @@
         dma = pltpu.SemaphoreType.DMA
         out, k_old, v_old, kv_new = pl.pallas_call(
             step_kernel,
-            out_shape=[pltpu.VMEM((ROWS, DIM), BF16), pltpu.VMEM(flat, BF16), pltpu.VMEM(flat, BF16),
+            out_shape=[pltpu.VMEM((ROWS, BLK), BF16), pltpu.VMEM(flat, BF16), pltpu.VMEM(flat, BF16),
                        pltpu.VMEM((2, ROWS, HD), F32)],
             in_specs=[pl.BlockSpec(memory_space=pltpu.HBM)] * 9,
             out_specs=[vm, vm, vm, vm],
@@ -399,7 +451,8 @@
                 pltpu.SMEM((ROWS,), jnp.int32),
                 pltpu.VMEM((2, ROWS * HEADS, 128), F32),
                 pltpu.VMEM((NW, ROWS, HD), BF16),
-                pltpu.VMEM((NW, ROWS, HD), BF16),
+                pltpu.VMEM((NW + SHARED, ROWS, HD), BF16),
+                pltpu.VMEM((SHARED, ROWS, HD), BF16),
                 pltpu.VMEM((CHUNK * HEADS, SEQ), BF16),
                 pltpu.VMEM((CHUNK * HEADS, 128), F32),
                 pltpu.VMEM((2, NCH, 2, CR, HD), F32),
@@ -410,24 +463,24 @@
                 pltpu.VMEM((NCH, 8, 128), F32),
                 pltpu.VMEM((2, 4 * ROWS, 128), F32),
                 pltpu.VMEM((ROWS, BLK), BF16),
-                pltpu.VMEM((2, 2, HALF, BLK), F32),
-                pltpu.VMEM((2, HALF, BLK), F32),
-                pltpu.VMEM((2, HALF, BLK), F32),
-                pltpu.VMEM((2, 2, HALF, BLK), F32),
-                pltpu.VMEM((2, HALF, BLK), F32),
-                pltpu.VMEM((4, ROWS, BLK), BF16),
+                pltpu.VMEM((NOUT, 2, OUT, BLK), F32),
+                pltpu.VMEM((NOUT, OUT, BLK), F32),
+                pltpu.VMEM((NOUT, OUT, BLK), F32),
+                pltpu.VMEM((NOUT, 2, OUT, BLK), F32),
+                pltpu.VMEM((NOUT, OUT, BLK), F32),
                 dma((3,)), dma((NW,)), dma((8,)), dma((8,)), dma((4,)),
-                dma((NW,)), dma((NW,)),
+                dma((NW + SHARED,)), dma((NW + SHARED,)), dma((SHARED,)), dma((SHARED,)),
                 dma((NCH,)), dma((NCH,)), dma((NCH,)), dma((NCH,)),
                 dma((NCH,)), dma((NCH,)), dma((NCH,)), dma((NCH,)),
-                dma((4,)), dma((4,)), dma((2,)), dma((2,)),
-                dma((2,)), dma((2,)), dma((2,)), dma((2,)), dma((2,)), dma((2,)),
+                dma((2 * NOUT,)), dma((2 * NOUT,)), dma((NOUT,)), dma((NOUT,)),
             ],
             compiler_params=pltpu.CompilerParams(
                 vmem_limit_bytes=44 * 2 ** 20, collective_id=0, has_side_effects=True),
             name='decode_step',
         )(*args)
         anywhere = pl.BlockSpec(memory_space=pltpu.HBM)
+        others = [lax.ppermute(out, 'sp', [(i, i ^ j) for i in range(4)]) for j in (1, 2, 3)]
+        others = [pltpu.with_memory_space_constraint(o, pltpu.VMEM) for o in others]
         _, _, k_new, v_new = pl.pallas_call(
             cache_kernel,
             out_shape=[pltpu.VMEM(flat, BF16), pltpu.VMEM(flat, BF16),
@@ -436,9 +489,19 @@
             out_specs=[vm, vm, anywhere, anywhere],
             scratch_shapes=[dma((8,)), dma((8,))],
             input_output_aliases={2: 0, 3: 1},
+            cost_estimate=pl.CostEstimate(flops=2 ** 33, bytes_accessed=2 ** 25, transcendentals=0),
             compiler_params=pltpu.CompilerParams(vmem_limit_bytes=2 ** 20),
             name='cache_update',
         )(write_pos, kv_new, k_old, v_old)
-        return out, k_new.reshape(k_cache.shape), v_new.reshape(v_cache.shape)
+        attn_out = pl.pallas_call(
+            join_kernel,
+            out_shape=pltpu.HBM((ROWS, DIM), BF16),
+            in_specs=[vm] * 4,
+            out_specs=anywhere,
+            scratch_shapes=[dma((4,))],
+            compiler_params=pltpu.CompilerParams(vmem_limit_bytes=2 ** 20),
+            name='join',
+        )(out, *others)
+        return attn_out, k_new.reshape(k_cache.shape), v_new.reshape(v_cache.shape)
 
     return jax.shard_map(local_step, mesh=mesh, in_specs=(row_spec, P(), P(), P(), P('sp', None), cache_spec, cache_spec, len_spec, len_spec), out_specs=(row_spec, cache_spec, cache_spec), check_vma=False)

time: 43.4 us -> 37.9 us (0.87)
  Pallas kernels: 41.8 us -> 35.2 us
  starting transfers between devices: 0 us -> 1.88 us
  local copies, waits for them, and re-layouts: 0.8 us -> 0.01 us
    pallas_call x1 -> x2, Pallas kernels: 34.8 us -> 28.6 us  [the longest x1 27.7 us: local_step(): pl.pallas_call(step_kernel, out_shape=[pltpu.VMEM((ROWS, BLK), BF16), plt...]
    ppermute x0 -> x3, starting transfers between devices: none -> 1.88 us  [local_step(): lax.ppermute(out, 'sp', [(i, i ^ j) for i in range(4)])]
    unnamed x3 -> x2, local copies, waits for them, and re-layouts: 0.8 us -> 0.01 us
    pallas_call x1, Pallas kernels: 7.08 us -> 6.63 us  [local_step(): pl.pallas_call(cache_kernel, out_shape=[pltpu.VMEM(flat, BF16), pltpu.VME...]
  transfers between devices with their start and end apart: 0 -> 3, of which waited for: 0 -> 0; matrix products, arithmetic and copies ran while one was open for 0% -> 0% of each run, Pallas kernels for 0% -> 18%
where the time goes in v3:
time: 37.9 us; the launch traced here: 37.8 us
  Pallas kernels  35.2 us (93%)
  starting transfers between devices  1.88 us (5%)
  between operations  0.68 us (2%)
    pallas_call x1, Pallas kernels, local_step(): pl.pallas_call(step_kernel, out_shape=[pltpu.VMEM((ROWS, BLK), BF16), plt...  27.7 us
    pallas_call x1, Pallas kernels, local_step(): pl.pallas_call(cache_kernel, out_shape=[pltpu.VMEM(flat, BF16), pltpu.VME...  6.63 us
    ppermute x3, starting transfers between devices, local_step(): lax.ppermute(out, 'sp', [(i, i ^ j) for i in range(4)])  1.88 us
    pallas_call x1, Pallas kernels, local_step(): pl.pallas_call(join_kernel, out_shape=pltpu.HBM((ROWS, DIM), BF16), in_sp...  0.84 us
  transfers between devices with their start and end apart: 3, of which 0 were waited for; matrix products, arithmetic and copies ran while one was open for 0% of the time, Pallas kernels for 18%

profile of v3, /device:TPU:0, one launch (start us, length us, event | category | flops | bytes accessed | tf_op | source)
XLA Modules:
  0.0 37.8 jit_solution(13490570373665255100)
XLA Ops:
  0.6 0.0 copy-start
  0.6 27.7 %decode_step.1 = (bf16[64,1024]{1,0:T(8,128)(2,1)S(1)}, bf16[16384,256]{1,0:T(8,128)(2,1)S(1)}, bf16[16384,256]{1,0:T(8,128)(2,1)S(1)}, f32[2,64,256]{2,1,0:T(8,128)S(1)}) custom-call(bf16[64,4096]{1,0:T(8,128)(2,1)} %hid_hbm.1, bf16[4096,4096]{1,0:T(8,128)(2,1)} %wq_hbm.1, bf16[4096,256]{1,0:T(8,128)(2,1)} %wk_hbm.1, bf16[4096,256]{1,0:T(8,128)(2,1)} %wv_hbm.1, ...), custom_call_target="tpu_custom_call" | custom-call | tf_op jit(solution)/shard_map/decode_step/pallas_call | solution.py:440
  28.4 0.5 %collective-permute-start.2 = (bf16[64,1024]{1,0:T(8,128)(2,1)S(1)}, bf16[64,1024]{1,0:T(8,128)(2,1)S(1)}, u32[]{:S(2)}, u32[]{:S(2)}) collective-permute-start(bf16[64,1024]{1,0:T(8,128)(2,1)S(1)} %get-tuple-element.9.b0), channel_id=1, source_target_pairs={{0,3},{1,2},{2,1},{3,0},{4,7},{5,6},{6,5},{7,4}} | collective-permute-start | bytes 393224 | tf_op jit(solution)/shard_map/ppermute | solution.py:482
  28.9 0.9 %collective-permute-start.1 = (bf16[64,1024]{1,0:T(8,128)(2,1)S(1)}, bf16[64,1024]{1,0:T(8,128)(2,1)S(1)}, u32[]{:S(2)}, u32[]{:S(2)}) collective-permute-start(bf16[64,1024]{1,0:T(8,128)(2,1)S(1)} %get-tuple-element.9.b0), channel_id=1, source_target_pairs={{0,2},{1,3},{2,0},{3,1},{4,6},{5,7},{6,4},{7,5}} | collective-permute-start | bytes 393224 | tf_op jit(solution)/shard_map/ppermute | solution.py:482
  29.8 0.5 %collective-permute-start = (bf16[64,1024]{1,0:T(8,128)(2,1)S(1)}, bf16[64,1024]{1,0:T(8,128)(2,1)S(1)}, u32[]{:S(2)}, u32[]{:S(2)}) collective-permute-start(bf16[64,1024]{1,0:T(8,128)(2,1)S(1)} %get-tuple-element.9.b0), channel_id=1, source_target_pairs={{0,1},{1,0},{2,3},{3,2},{4,5},{5,4},{6,7},{7,6}} | collective-permute-start | bytes 393224 | tf_op jit(solution)/shard_map/ppermute | solution.py:482
  30.3 0.0 copy-done
  30.3 6.6 %cache_update.1 = (bf16[16384,256]{1,0:T(8,128)(2,1)S(1)}, bf16[16384,256]{1,0:T(8,128)(2,1)S(1)}, bf16[16384,256]{1,0:T(8,128)(2,1)}, bf16[16384,256]{1,0:T(8,128)(2,1)}) custom-call(s32[64]{0:T(128)S(1)} %copy-done, f32[2,64,256]{2,1,0:T(8,128)S(1)} %get-tuple-element.10.kvn, ...), custom_call_target="tpu_custom_call", output_to_operand_aliasing={{0}: (2, {}), {1}: (3, {})} | custom-call | flops 8589934592 | bytes 33554432 | tf_op jit(solution)/shard_map/cache_update/pallas_call | solution.py:484
  36.9 0.0 collective-permute-done.2.b3
  36.9 0.0 collective-permute-done.1.b2
  36.9 0.0 collective-permute-done.b1
  37.0 0.8 %join.1 = bf16[64,4096]{1,0:T(8,128)(2,1)} custom-call(bf16[64,1024]{1,0:T(8,128)(2,1)S(1)} %get-tuple-element.9.b0, bf16[64,1024]{1,0:T(8,128)(2,1)S(1)} %collective-permute-done.b1, bf16[64,1024]{1,0:T(8,128)(2,1)S(1)} %collective-permute-done.1.b2, bf16[64,1024]{1,0:T(8,128)(2,1)S(1)} %collective-permute-done.2.b3), custom_call_target="tpu_custom_call" | custom-call | tf_op jit(solution)/shard_map/join/pallas_call | solution.py:496
Async XLA Ops:
  0.6 29.6 %copy-start = (s32[64]{0:T(128)S(1)}, s32[64]{0:T(128)}, u32[]{:S(2)}) copy-start(s32[64]{0:T(128)} %wp.1) | copy-start | bytes 772
  28.4 8.5 %collective-permute-start.2 = (bf16[64,1024]{1,0:T(8,128)(2,1)S(1)}, bf16[64,1024]{1,0:T(8,128)(2,1)S(1)}, u32[]{:S(2)}, u32[]{:S(2)}) collective-permute-start(bf16[64,1024]{1,0:T(8,128)(2,1)S(1)} %get-tuple-element.9.b0), channel_id=1, source_target_pairs={{0,3},{1,2},{2,1},{3,0},{4,7},{5,6},{6,5},{7,4}} | collective-permute-start | bytes 393224 | tf_op jit(solution)/shard_map/ppermute | solution.py:482
  28.9 8.1 %collective-permute-start.1 = (bf16[64,1024]{1,0:T(8,128)(2,1)S(1)}, bf16[64,1024]{1,0:T(8,128)(2,1)S(1)}, u32[]{:S(2)}, u32[]{:S(2)}) collective-permute-start(bf16[64,1024]{1,0:T(8,128)(2,1)S(1)} %get-tuple-element.9.b0), channel_id=1, source_target_pairs={{0,2},{1,3},{2,0},{3,1},{4,6},{5,7},{6,4},{7,5}} | collective-permute-start | bytes 393224 | tf_op jit(solution)/shard_map/ppermute | solution.py:482
  29.8 7.2 %collective-permute-start = (bf16[64,1024]{1,0:T(8,128)(2,1)S(1)}, bf16[64,1024]{1,0:T(8,128)(2,1)S(1)}, u32[]{:S(2)}, u32[]{:S(2)}) collective-permute-start(bf16[64,1024]{1,0:T(8,128)(2,1)S(1)} %get-tuple-element.9.b0), channel_id=1, source_target_pairs={{0,1},{1,0},{2,3},{3,2},{4,5},{5,4},{6,7},{7,6}} | collective-permute-start | bytes 393224 | tf_op jit(solution)/shard_map/ppermute | solution.py:482

commit v4 on v3

v4 whole, which is shorter than its diff:
```python
import jax
import jax.numpy as jnp
from jax import lax
from jax.experimental import pallas as pl
from jax.experimental.pallas import tpu as pltpu
from jax.sharding import PartitionSpec as P

MESH = pl.DeviceIdType.MESH
F32, BF16 = jnp.float32, jnp.bfloat16
LOWEST = float(jnp.finfo(jnp.float32).min)

ROWS = 64
SEQ = 256
DIM = 4096
HD = 256
HEADS = 16
GROUP = 8
CHUNK = 16
NCH = ROWS // CHUNK
NPAIR = CHUNK // 2
CR = NPAIR * 8
OUT = 16
NOUT = ROWS // OUT
BLK = 1024
SPLIT = 5
AHEAD = 4
SHARED = 3
RELAY = 2
NOWN = 8 - SHARED
NW = NOWN + 1
DIST = 1


def step_kernel(hid_hbm, wq_hbm, wk_hbm, wv_hbm, wo_hbm, kc_hbm, vc_hbm, wp_hbm, vl_hbm,
                out_ref, k_ref, v_ref, kvn, wp,
                hid, wbuf, wo, vl, qf, qsend, qrecv, qchip, prob, pnew,
                acc, racc1, racc2, rml2, osum, obf,
                pd, rd, px, rx, pn, rn, pk,
                s_in, s_w, s_k, s_v, s_wo,
                qs, qr, qxs, qxr, qrs, qrr, a1s, a1r, a2s, a2r, m2s, m2r,
                f_s, f_r, n_s, n_r, rxs, rxr):
    sp = lax.axis_index('sp')
    x, c = sp // 2, sp % 2
    sib = 2 * x + (1 - c)
    xp = 2 * (1 - x) + c
    diag = 2 * (1 - x) + 1 - c
    first_pos = sp * SEQ

    def remote(src, dst, ss, rs, peer):
        return pltpu.make_async_remote_copy(src_ref=src, dst_ref=dst, send_sem=ss, recv_sem=rs,
                                            device_id={'sp': peer}, device_id_type=MESH)

    hid_cp = pltpu.make_async_copy(hid_hbm, hid, s_in.at[0])
    wp_cp = pltpu.make_async_copy(wp_hbm, wp, s_in.at[1])
    vl_cp = pltpu.make_async_copy(vl_hbm, vl, s_in.at[2])
    hid_cp.start()

    def head(i, chip):
        return i + chip * (7 - 2 * i)

    def wq_cp(i):
        cols = pl.ds(pl.multiple_of((8 * c + head(i, x)) * HD, HD), HD)
        return pltpu.make_async_copy(wq_hbm.at[:, cols], wbuf.at[i], s_w.at[i % AHEAD])

    def k_cp(g):
        rows = pl.ds(g * CHUNK * SEQ, CHUNK * SEQ)
        return pltpu.make_async_copy(kc_hbm.at[rows], k_ref.at[rows], s_k.at[g])

    def v_cp(g):
        rows = pl.ds(g * CHUNK * SEQ, CHUNK * SEQ)
        return pltpu.make_async_copy(vc_hbm.at[rows], v_ref.at[rows], s_v.at[g])

    def wo_cp(i):
        rows = pl.ds(i * 256, 256)
        return pltpu.make_async_copy(wo_hbm.at[rows], wo.at[rows], s_wo.at[0])

    def start_w(i):
        @pl.when(i < NOWN)
        def _():
            wq_cp(i).start()

        @pl.when((i == NOWN) & (c == 0))
        def _():
            pltpu.make_async_copy(wk_hbm, wbuf.at[NOWN], s_w.at[NOWN % AHEAD]).start()

        @pl.when((i == NOWN) & (c == 1))
        def _():
            pltpu.make_async_copy(wv_hbm, wbuf.at[NOWN], s_w.at[NOWN % AHEAD]).start()

        @pl.when((i > NOWN) & (i < NW + NCH))
        def _():
            k_cp(i - NW).start()
            v_cp(i - NW).start()

    for i in range(AHEAD):
        wq_cp(i).start()
    wp_cp.start()
    vl_cp.start()

    barrier = pltpu.get_barrier_semaphore()
    for peer in (sib, xp, diag):
        pl.semaphore_signal(barrier, inc=1, device_id={'sp': peer}, device_id_type=MESH)

    hid_cp.wait()
    pl.semaphore_wait(barrier, 3)

    def spread(slot, q):
        for h in range(2):
            qf[h, pl.ds(slot, ROWS, stride=HEADS), :] = q[:, h * 128:(h + 1) * 128]

    def slot(i, chip, core):
        h = head(i, chip)
        return 8 * (h // 4) + 4 * core + h % 4

    def q_core(i):
        return remote(qsend.at[i], qrecv.at[i], qs.at[0], qr.at[0], sib)

    def q_chip(i):
        return remote(qsend.at[i], qchip.at[i], qxs.at[0], qxr.at[i], xp)

    def q_far(i):
        return remote(qsend.at[i], qrecv.at[NW + i], qxs.at[0], qrr.at[0], diag)

    def q_relay(i):
        return remote(qchip.at[i], qrecv.at[NW + i], qrs.at[0], qrr.at[0], sib)

    def project(i):
        pltpu.make_async_copy(wk_hbm, wbuf.at[i], s_w.at[i % AHEAD]).wait()
        start_w(i + AHEAD)
        res = jnp.dot(hid[...], wbuf[i], preferred_element_type=F32).astype(BF16)
        qsend[i] = res
        q_core(i).start()
        return res.astype(F32)

    def head_step(i, _):
        res = project(i)

        @pl.when(i < SHARED)
        def _():
            q_chip(i).start()

        @pl.when((i >= RELAY) & (i < SHARED))
        def _():
            q_far(i).start()

        spread(slot(i, x, c), res)
        return 0

    lax.fori_loop(0, NOWN, head_step, 0)
    for g in range(NCH + NW - AHEAD - NW, NCH):
        if g + NW >= NW + AHEAD:
            k_cp(g).start()
            v_cp(g).start()
    kvn[c] = project(NOWN)
    for i in range(RELAY):
        q_chip(i).wait_recv()
        q_relay(i).start()
    for i in range(SHARED):
        if i >= RELAY:
            q_chip(i).wait_recv()
        spread(slot(i, 1 - x, c), qchip[i].astype(F32))
    remote(qsend, qrecv.at[pl.ds(0, NW)], qs.at[0], qr.at[0], sib).wait_recv()
    kvn[1 - c] = qrecv[NOWN].astype(F32)

    def take_head(i, _):
        spread(slot(i, x, 1 - c), qrecv[i].astype(F32))
        return 0

    lax.fori_loop(0, NOWN, take_head, 0)
    remote(qchip, qrecv.at[pl.ds(NW, SHARED)], qrs.at[0], qrr.at[0], sib).wait_recv()
    for i in range(SHARED):
        spread(slot(i, 1 - x, 1 - c), qrecv[NW + i].astype(F32))
    wp_cp.wait()
    vl_cp.wait()

    sub = lax.broadcasted_iota(jnp.int32, (8, HD), 0)
    sub1 = lax.broadcasted_iota(jnp.int32, (8, 128), 0)
    lane1 = lax.broadcasted_iota(jnp.int32, (8, 128), 1)
    lane = lax.broadcasted_iota(jnp.int32, (HEADS, SEQ), 1)

    def cache_rows(b):
        return pl.ds(pl.multiple_of(b * SEQ, SEQ), SEQ)

    def weigh(b, j):
        rows = pl.ds(pl.multiple_of(b * HEADS, HEADS), HEADS)
        q = jnp.concatenate([qf[0, rows, :], qf[1, rows, :]], axis=1)
        s = lax.dot_general(q.astype(BF16), k_ref[cache_rows(b), :], (((1,), (1,)), ((), ())),
                            preferred_element_type=F32)
        s_new = jnp.sum(q * kvn[0, pl.ds(b, 1), :], axis=1, keepdims=True)
        here = lane == wp[b] - first_pos
        s = jnp.where(here, s_new, s) * (HD ** -0.5)
        s = jnp.where(lane < vl[b] - first_pos, s, -jnp.inf)
        m = jnp.maximum(jnp.max(s, axis=1, keepdims=True), LOWEST)
        p = jnp.exp(s - m)
        l = jnp.sum(p, axis=1, keepdims=True)
        p_new = jnp.sum(jnp.where(here, p, 0.0), axis=1, keepdims=True)
        mine = slice(j * HEADS, (j + 1) * HEADS)
        prob[mine, :] = jnp.where(here, 0.0, p).astype(BF16)
        pnew[mine, :] = jnp.broadcast_to(p_new, (HEADS, 128))
        return jnp.broadcast_to(m, (HEADS, 128)), jnp.broadcast_to(l, (HEADS, 128))

    def value_sum(b, j):
        mine = slice(j * HEADS, (j + 1) * HEADS)
        o = jnp.dot(prob[mine, :], v_ref[cache_rows(b), :], preferred_element_type=F32)
        p_new = pnew[mine, :]
        return o + jnp.concatenate([p_new, p_new], axis=1) * kvn[1, pl.ds(b, 1), :]

    def pack(t0, t1, low):
        return (jnp.where(low, t0, pltpu.roll(t1, 4, 0)), jnp.where(low, pltpu.roll(t0, 4, 0), t1))

    def chunk_attention(ch, between):
        k_cp(ch).wait()

        @pl.when(ch >= 0)
        def _():
            tiles = [jnp.zeros((8, 128), F32)] * 4
            for p in range(NPAIR):
                m0, l0 = weigh(ch * CHUNK + 2 * p, 2 * p)
                m1, l1 = weigh(ch * CHUNK + 2 * p + 1, 2 * p + 1)
                for core in range(2):
                    r = slice(8 * core, 8 * core + 8)
                    ms = pack(m0[r], m1[r], sub1 < 4)
                    ls = pack(l0[r], l1[r], sub1 < 4)
                    for xd in range(2):
                        t = jnp.where(lane1 == p, ms[xd], tiles[2 * core + xd])
                        tiles[2 * core + xd] = jnp.where(lane1 == p + 64, ls[xd], t)
            for core in range(2):
                acc[core, ch, 2 * CR:, :] = jnp.concatenate(tiles[2 * core:2 * core + 2], axis=1)

        v_cp(ch).wait()

        @pl.when(ch >= 0)
        def _():
            for p in range(NPAIR):
                o0 = value_sum(ch * CHUNK + 2 * p, 2 * p)
                o1 = value_sum(ch * CHUNK + 2 * p + 1, 2 * p + 1)
                for core in range(2):
                    r = slice(8 * core, 8 * core + 8)
                    os = pack(o0[r], o1[r], sub < 4)
                    for xd in range(2):
                        acc[core, ch, xd * CR + p * 8:xd * CR + p * 8 + 8, :] = os[xd]

    def d2d(ch):
        return remote(acc.at[1 - c, ch], racc1.at[ch], a1s.at[0], a1r.at[ch], sib)

    def xlink(ch):
        sums = pl.ds(pl.multiple_of((1 - x) * CR, 8), CR)
        lanes = pl.ds(pl.multiple_of((1 - x) * 128, 128), 128)
        return (remote(acc.at[c, ch, sums], racc2.at[ch], a2s.at[0], a2r.at[ch], xp),
                remote(acc.at[c, ch, pl.ds(2 * CR, 8), lanes], rml2.at[ch], m2s.at[0], m2r.at[ch], xp))

    def scales(mla, mlb):
        top = jnp.maximum(mla, mlb)
        sa, sb = jnp.exp(mla - top), jnp.exp(mlb - top)
        total = mla * pltpu.roll(sa, 64, 1) + mlb * pltpu.roll(sb, 64, 1)
        return top, sa, sb, total

    def merge_core(ch):
        d2d(ch).wait_recv()
        for xd in range(2):
            lanes = slice(xd * 128, xd * 128 + 128)
            top, sa, sb, total = scales(acc[c, ch, 2 * CR:, lanes], racc1[ch, 2 * CR:, lanes])
            acc[c, ch, 2 * CR:, lanes] = jnp.where(lane1 < 64, top, total)
            for p in range(NPAIR):
                r = slice(xd * CR + p * 8, xd * CR + p * 8 + 8)
                acc[c, ch, r, :] = acc[c, ch, r, :] * sa[:, p:p + 1] + racc1[ch, r, :] * sb[:, p:p + 1]
        for desc in xlink(ch):
            desc.start()

    def merge_chip(ch):
        for desc in xlink(ch):
            desc.wait_recv()
        lanes = pl.ds(pl.multiple_of(x * 128, 128), 128)
        top, sa, sb, total = scales(acc[c, ch, 2 * CR:, lanes], rml2[ch])
        inv = pltpu.roll(1.0 / jnp.where(lane1 < 64, 1.0, total), 64, 1)
        sa, sb = sa * inv, sb * inv
        for p in range(NPAIR):
            mine = pl.ds(pl.multiple_of(x * CR + p * 8, 8), 8)
            o = acc[c, ch, mine, :] * sa[:, p:p + 1] + racc2[ch, p * 8:p * 8 + 8, :] * sb[:, p:p + 1]
            for h in range(2):
                osum[h, pl.ds(pl.multiple_of(ch * CR + p * 8, 8), 8), :] = o[:, h * 128:(h + 1) * 128]

    def far_sum(t):
        return remote(pd.at[t], rd.at[t], f_s.at[0], f_r.at[t], sib)

    def near_sum():
        return remote(pn, rn, n_s.at[0], n_r.at[0], sib)

    def chip_sum(t):
        return remote(px.at[t], rx.at[t], rxs.at[0], rxr.at[0], xp)

    def project_block(dst, rows, j):
        cols = pl.ds(pl.multiple_of(j * BLK, BLK), BLK)
        dst[...] = jnp.dot(obf[rows, :], wo[:, cols], preferred_element_type=F32)

    def project_far(t):
        rows = pl.ds(pl.multiple_of(t * OUT, OUT), OUT)
        for r in range(4):
            for h in range(2):
                lanes = slice(r * HD + h * 128, r * HD + (h + 1) * 128)
                obf[rows, lanes] = osum[h, pl.ds(t * 4 * OUT + r, OUT, stride=4), :].astype(BF16)
        project_block(pd.at[t], rows, diag)
        project_block(px.at[t], rows, xp)
        far_sum(t).start()

    def project_near():
        project_block(pn, pl.ds(0, ROWS), sib)
        project_block(pk, pl.ds(0, ROWS), sp)
        near_sum().start()

    def send_far(t):
        far_sum(t).wait_recv()
        px[t] = px[t] + rd[t]
        chip_sum(t).start()

    def pipeline(ch, _):
        def earlier():
            @pl.when(ch >= DIST)
            def _():
                merge_core(ch - DIST)

        @pl.when(ch < 4)
        def _():
            wo_cp(ch).start()

        chunk_attention(ch, earlier)
        d2d(ch).start()
        earlier()
        return 0

    lax.fori_loop(0, NCH, pipeline, 0)

    pltpu.make_async_copy(wo_hbm, wo, s_wo.at[0]).wait()

    def outputs(t, _):
        for u in range(OUT // CHUNK):
            merge_chip(t * (OUT // CHUNK) + u)
        project_far(t)

        @pl.when(t > 0)
        def _():
            send_far(t - 1)
        return 0

    merge_core(NCH - 1)
    lax.fori_loop(0, NOUT, outputs, 0)
    project_near()
    send_far(NOUT - 1)

    remote(qsend, qrecv.at[pl.ds(0, NW)], qs.at[0], qr.at[0], sib).wait_send()
    n_far = 2 * SHARED - RELAY
    remote(qrecv.at[pl.ds(0, n_far)], qrecv.at[pl.ds(0, n_far)], qxs.at[0], qxr.at[0], xp).wait_send()
    remote(qchip.at[pl.ds(0, RELAY)], qrecv.at[pl.ds(0, RELAY)], qrs.at[0], qrr.at[0], sib).wait_send()
    remote(acc.at[1 - c], racc1, a1s.at[0], a1r.at[0], sib).wait_send()
    remote(racc2, racc2, a2s.at[0], a2r.at[0], xp).wait_send()
    remote(rml2, rml2, m2s.at[0], m2r.at[0], xp).wait_send()
    remote(px, rx, f_s.at[0], f_r.at[0], sib).wait_send()
    near_sum().wait_send()

    near_sum().wait_recv()
    remote(px, rx, rxs.at[0], rxr.at[0], xp).wait_recv()
    for t in range(NOUT):
        r = slice(t * OUT, (t + 1) * OUT)
        out_ref[r, :] = ((pk[r, :] + rn[r, :]) + rx[t]).astype(BF16)
    remote(px, rx, rxs.at[0], rxr.at[0], xp).wait_send()


def insert_rows(wp, kvn, first_pos, ref, i, groups):
    row = lax.broadcasted_iota(jnp.int32, (16, HD), 0)
    for b in range(groups.start * GROUP, groups.stop * GROUP):
        pos = wp[b] - first_pos
        base = jnp.clip(pos, 0, SEQ - 1) // 16 * 16
        rows = pl.ds(pl.multiple_of(b * SEQ + base, 16), 16)
        ref[rows, :] = jnp.where(row == pos - base, kvn[i, pl.ds(b, 1), :], ref[rows, :].astype(F32)).astype(BF16)


def copy_group(ref, out, sem, g):
    rows = pl.ds(g * GROUP * SEQ, GROUP * SEQ)
    return pltpu.make_async_copy(ref.at[rows], out.at[rows], sem)


def cache_kernel(wp, kvn, k_in, v_in, k_ref, v_ref, k_out, v_out, sems):
    first_pos = lax.axis_index('sp') * SEQ
    copies = []
    for g in range(9):
        if g < 8:
            insert_rows(wp, kvn, first_pos, k_ref, 0, range(g, g + 1))
            insert_rows(wp, kvn, first_pos, v_ref, 1, range(g, g + 1))
        if g >= 1:
            copies.append(copy_group(k_ref, k_out, sems.at[len(copies)], g - 1))
            copies[-1].start()
            if g <= SPLIT:
                copies.append(copy_group(v_ref, v_out, sems.at[len(copies)], g - 1))
                copies[-1].start()
    for cp in copies:
        cp.wait()


def rest_kernel(v_ref, token, v_in, v_out, sems):
    copies = [copy_group(v_ref, v_out, sems.at[g], g) for g in range(SPLIT, 8)]
    for cp in copies:
        cp.start()
    for cp in copies:
        cp.wait()


def join_kernel(b0, b1, b2, b3, out, sems):
    sp = lax.axis_index('sp')
    x, c = sp // 2, sp % 2
    copies = []
    for i, ref in enumerate((b0, b1, b2, b3)):
        j = 2 * (x if i < 2 else 1 - x) + (c if i % 2 == 0 else 1 - c)
        cols = pl.ds(pl.multiple_of(j * BLK, BLK), BLK)
        copies.append(pltpu.make_async_copy(ref, out.at[:, cols], sems.at[i]))
    for cp in copies:
        cp.start()
    for cp in copies:
        cp.wait()


def solution(mesh):
    row_spec = P(('rep', 'dp'), None)
    cache_spec = P(('rep', 'dp'), 'sp', None, None)
    len_spec = P(('rep', 'dp'))

    def local_step(hidden, w_query, w_key, w_value, w_out, k_cache, v_cache, write_pos, valid_len):
        flat = (ROWS * SEQ, HD)
        args = (hidden, w_query, w_key, w_value, w_out, k_cache.reshape(flat), v_cache.reshape(flat),
                write_pos, valid_len)
        args = tuple(pltpu.with_memory_space_constraint(a, pltpu.HBM) for a in args)
        vm = pl.BlockSpec(memory_space=pltpu.VMEM)
        dma = pltpu.SemaphoreType.DMA
        out, k_old, v_old, kv_new, where_to = pl.pallas_call(
            step_kernel,
            out_shape=[pltpu.VMEM((ROWS, BLK), BF16), pltpu.VMEM(flat, BF16), pltpu.VMEM(flat, BF16),
                       pltpu.VMEM((2, ROWS, HD), F32), pltpu.SMEM((ROWS,), jnp.int32)],
            in_specs=[pl.BlockSpec(memory_space=pltpu.HBM)] * 9,
            out_specs=[vm, vm, vm, vm, pl.BlockSpec(memory_space=pltpu.SMEM)],
            scratch_shapes=[
                pltpu.VMEM((ROWS, DIM), BF16),
                pltpu.VMEM((NW, DIM, HD), BF16),
                pltpu.VMEM((BLK, DIM), BF16),
                pltpu.SMEM((ROWS,), jnp.int32),
                pltpu.VMEM((2, ROWS * HEADS, 128), F32),
                pltpu.VMEM((NW, ROWS, HD), BF16),
                pltpu.VMEM((NW + SHARED, ROWS, HD), BF16),
                pltpu.VMEM((SHARED, ROWS, HD), BF16),
                pltpu.VMEM((CHUNK * HEADS, SEQ), BF16),
                pltpu.VMEM((CHUNK * HEADS, 128), F32),
                pltpu.VMEM((2, NCH, 2 * CR + 8, HD), F32),
                pltpu.VMEM((NCH, 2 * CR + 8, HD), F32),
                pltpu.VMEM((NCH, CR, HD), F32),
                pltpu.VMEM((NCH, 8, 128), F32),
                pltpu.VMEM((2, 4 * ROWS, 128), F32),
                pltpu.VMEM((ROWS, BLK), BF16),
                pltpu.VMEM((NOUT, OUT, BLK), F32),
                pltpu.VMEM((NOUT, OUT, BLK), F32),
                pltpu.VMEM((NOUT, OUT, BLK), F32),
                pltpu.VMEM((NOUT, OUT, BLK), F32),
                pltpu.VMEM((ROWS, BLK), F32),
                pltpu.VMEM((ROWS, BLK), F32),
                pltpu.VMEM((ROWS, BLK), F32),
                dma((3,)), dma((AHEAD,)), dma((NCH,)), dma((NCH,)), dma((1,)),
                dma((1,)), dma((1,)), dma((1,)), dma((SHARED,)), dma((1,)), dma((1,)),
                dma((1,)), dma((NCH,)), dma((1,)), dma((NCH,)), dma((1,)), dma((NCH,)),
                dma((1,)), dma((NOUT,)), dma((1,)), dma((1,)), dma((1,)), dma((1,)),
            ],
            compiler_params=pltpu.CompilerParams(
                vmem_limit_bytes=44 * 2 ** 20, collective_id=0, has_side_effects=True),
            name='decode_step',
        )(*args)
        anywhere = pl.BlockSpec(memory_space=pltpu.HBM)
        near = [(i, i ^ 1) for i in range(4)]
        chip = lax.ppermute(out, 'sp', [(i, i ^ 2) for i in range(4)])
        core = lax.ppermute(out, 'sp', near)
        far = lax.ppermute(chip, 'sp', near)
        k_full, v_full, k_new, v_new = pl.pallas_call(
            cache_kernel,
            out_shape=[pltpu.VMEM(flat, BF16), pltpu.VMEM(flat, BF16),
                       pltpu.HBM(flat, BF16), pltpu.HBM(flat, BF16)],
            in_specs=[pl.BlockSpec(memory_space=pltpu.SMEM), vm, vm, vm],
            out_specs=[vm, vm, anywhere, anywhere],
            scratch_shapes=[dma((16,))],
            input_output_aliases={2: 0, 3: 1},
            cost_estimate=pl.CostEstimate(flops=2 ** 33, bytes_accessed=2 ** 25, transcendentals=0),
            compiler_params=pltpu.CompilerParams(vmem_limit_bytes=2 ** 20),
            name='cache_update',
        )(where_to, kv_new, k_old, v_old)
        v_new = pl.pallas_call(
            rest_kernel,
            out_shape=pltpu.HBM(flat, BF16),
            in_specs=[vm, pl.BlockSpec(memory_space=pl.ANY), anywhere],
            out_specs=anywhere,
            scratch_shapes=[dma((8,))],
            input_output_aliases={2: 0},
            cost_estimate=pl.CostEstimate(flops=2 ** 33, bytes_accessed=2 ** 24, transcendentals=0),
            compiler_params=pltpu.CompilerParams(vmem_limit_bytes=2 ** 20),
            name='cache_rest',
        )(v_full, chip, v_new)
        others = [pltpu.with_memory_space_constraint(o, pltpu.VMEM) for o in (core, chip, far)]
        attn_out = pl.pallas_call(
            join_kernel,
            out_shape=pltpu.HBM((ROWS, DIM), BF16),
            in_specs=[vm] * 4,
            out_specs=anywhere,
            scratch_shapes=[dma((4,))],
            compiler_params=pltpu.CompilerParams(vmem_limit_bytes=2 ** 20),
            name='join',
        )(out, *others)
        return attn_out, k_new.reshape(k_cache.shape), v_new.reshape(v_cache.shape)

    return jax.shard_map(local_step, mesh=mesh, in_specs=(row_spec, P(), P(), P(), P('sp', None), cache_spec, cache_spec, len_spec, len_spec), out_specs=(row_spec, cache_spec, cache_spec), check_vma=False)
```

time: 37.9 us -> 36.4 us (0.960)
  Pallas kernels: 35.2 us -> 34.2 us
  starting transfers between devices: 1.88 us -> 1.43 us
    pallas_call x0 -> x1, Pallas kernels: none -> 1.73 us  [local_step(): pl.pallas_call(rest_kernel, out_shape=pltpu.HBM(flat, BF16), in_specs=[vm...]
    pallas_call x1, Pallas kernels: 6.63 us -> 5.19 us  [local_step(): pl.pallas_call(cache_kernel, out_shape=[pltpu.VMEM(flat, BF16), pltpu.VME...]
    pallas_call x1, Pallas kernels: 27.7 us -> 26.5 us  [local_step(): pl.pallas_call(step_kernel, out_shape=[pltpu.VMEM((ROWS, BLK), BF16), plt...]
    ppermute x3, starting transfers between devices: 1.88 us -> 1.43 us  [the longest x1 0.9 us: local_step(): chip = lax.ppermute(out, 'sp', [(i, i ^ 2) for i in range(4)])]
  transfers between devices with their start and end apart: 3 -> 3, of which waited for: 0 -> 0; matrix products, arithmetic and copies ran while one was open for 0% -> 0% of each run, Pallas kernels for 18% -> 19%
where the time goes in v4:
time: 36.4 us; the launch traced here: 36.3 us
  Pallas kernels  34.2 us (94%)
  starting transfers between devices  1.43 us (4%)
  between operations  0.68 us (2%)
    pallas_call x1, Pallas kernels, local_step(): pl.pallas_call(step_kernel, out_shape=[pltpu.VMEM((ROWS, BLK), BF16), plt...  26.5 us
    pallas_call x1, Pallas kernels, local_step(): pl.pallas_call(cache_kernel, out_shape=[pltpu.VMEM(flat, BF16), pltpu.VME...  5.19 us
    pallas_call x1, Pallas kernels, local_step(): pl.pallas_call(rest_kernel, out_shape=pltpu.HBM(flat, BF16), in_specs=[vm...  1.73 us
    ppermute x1, starting transfers between devices, local_step(): chip = lax.ppermute(out, 'sp', [(i, i ^ 2) for i in range(4)])  0.9 us
    pallas_call x1, Pallas kernels, local_step(): pl.pallas_call(join_kernel, out_shape=pltpu.HBM((ROWS, DIM), BF16), in_sp...  0.84 us
  transfers between devices with their start and end apart: 3, of which 0 were waited for; matrix products, arithmetic and copies ran while one was open for 0% of the time, Pallas kernels for 19%

profile of v4, /device:TPU:0, one launch (start us, length us, event | category | flops | bytes accessed | tf_op | source)
XLA Modules:
  0.0 36.3 jit_solution(16105011794536973711)
XLA Ops:
  0.6 26.5 %decode_step.1 = (bf16[64,1024]{1,0:T(8,128)(2,1)S(1)}, bf16[16384,256]{1,0:T(8,128)(2,1)S(1)}, bf16[16384,256]{1,0:T(8,128)(2,1)S(1)}, f32[2,64,256]{2,1,0:T(8,128)S(1)}, s32[64]{0:T(128)S(4)}) custom-call(bf16[64,4096]{1,0:T(8,128)(2,1)} %hid_hbm.1, bf16[4096,4096]{1,0:T(8,128)(2,1)} %wq_hbm.1, bf16[4096,256]{1,0:T(8,128)(2,1)} %wk_hbm.1, ...), custom_call_target="tpu_custom_call" | custom-call | tf_op jit(solution)/shard_map/decode_step/pallas_call | solution.py:433
  27.1 0.9 %collective-permute-start.1 = (bf16[64,1024]{1,0:T(8,128)(2,1)S(1)}, bf16[64,1024]{1,0:T(8,128)(2,1)S(1)}, u32[]{:S(2)}, u32[]{:S(2)}) collective-permute-start(bf16[64,1024]{1,0:T(8,128)(2,1)S(1)} %get-tuple-element.11.b0), channel_id=1, source_target_pairs={{0,2},{1,3},{2,0},{3,1},{4,6},{5,7},{6,4},{7,5}} | collective-permute-start | bytes 393224 | tf_op jit(solution)/shard_map/ppermute | solution.py:474
  28.0 0.0 collective-permute-start
  28.0 5.2 %cache_update.1 = (bf16[16384,256]{1,0:T(8,128)(2,1)S(1)}, bf16[16384,256]{1,0:T(8,128)(2,1)S(1)}, bf16[16384,256]{1,0:T(8,128)(2,1)}, bf16[16384,256]{1,0:T(8,128)(2,1)}) custom-call(s32[64]{0:T(128)S(4)} %get-tuple-element.12.wp, f32[2,64,256]{2,1,0:T(8,128)S(1)} %get-tuple-element.13.kvn, ...), custom_call_target="tpu_custom_call", output_to_operand_aliasing={{0}: (2, {}), {1}: (3, {})} | custom-call | flops 8589934592 | bytes 33554432 | tf_op jit(solution)/shard_map/cache_update/pallas_call | solution.py:477
  33.2 0.0 collective-permute-done.1.b2.token
  33.2 0.5 %collective-permute-start.2 = (bf16[64,1024]{1,0:T(8,128)(2,1)S(1)}, bf16[64,1024]{1,0:T(8,128)(2,1)S(1)}, u32[]{:S(2)}, u32[]{:S(2)}) collective-permute-start(bf16[64,1024]{1,0:T(8,128)(2,1)S(1)} %collective-permute-done.1.b2.token), channel_id=1, source_target_pairs={{0,1},{1,0},{2,3},{3,2},{4,5},{5,4},{6,7},{7,6}} | collective-permute-start | bytes 393224 | tf_op jit(solution)/shard_map/ppermute | solution.py:476
  33.7 1.7 %cache_rest.1 = bf16[16384,256]{1,0:T(8,128)(2,1)} custom-call(bf16[16384,256]{1,0:T(8,128)(2,1)S(1)} %get-tuple-element.17.v_ref, bf16[64,1024]{1,0:T(8,128)(2,1)S(1)} %collective-permute-done.1.b2.token, bf16[16384,256]{1,0:T(8,128)(2,1)} %get-tuple-element.18.v_in), custom_call_target="tpu_custom_call", output_to_operand_aliasing={{}: (2, {})} | custom-call | flops 8589934592 | bytes 16777216 | tf_op jit(solution)/shard_map/cache_rest/pallas_call | solution.py:489
  35.5 0.0 collective-permute-done.b1
  35.5 0.0 collective-permute-done.2.b3
  35.5 0.8 %join.1 = bf16[64,4096]{1,0:T(8,128)(2,1)} custom-call(bf16[64,1024]{1,0:T(8,128)(2,1)S(1)} %get-tuple-element.11.b0, bf16[64,1024]{1,0:T(8,128)(2,1)S(1)} %collective-permute-done.b1, bf16[64,1024]{1,0:T(8,128)(2,1)S(1)} %collective-permute-done.1.b2.token, bf16[64,1024]{1,0:T(8,128)(2,1)S(1)} %collective-permute-done.2.b3), custom_call_target="tpu_custom_call" | custom-call | tf_op jit(solution)/shard_map/join/pallas_call | solution.py:501
Async XLA Ops:
  27.1 6.1 %collective-permute-start.1 = (bf16[64,1024]{1,0:T(8,128)(2,1)S(1)}, bf16[64,1024]{1,0:T(8,128)(2,1)S(1)}, u32[]{:S(2)}, u32[]{:S(2)}) collective-permute-start(bf16[64,1024]{1,0:T(8,128)(2,1)S(1)} %get-tuple-element.11.b0), channel_id=1, source_target_pairs={{0,2},{1,3},{2,0},{3,1},{4,6},{5,7},{6,4},{7,5}} | collective-permute-start | bytes 393224 | tf_op jit(solution)/shard_map/ppermute | solution.py:474
  28.0 7.5 %collective-permute-start = (bf16[64,1024]{1,0:T(8,128)(2,1)S(1)}, bf16[64,1024]{1,0:T(8,128)(2,1)S(1)}, u32[]{:S(2)}, u32[]{:S(2)}) collective-permute-start(bf16[64,1024]{1,0:T(8,128)(2,1)S(1)} %get-tuple-element.11.b0), channel_id=1, source_target_pairs={{0,1},{1,0},{2,3},{3,2},{4,5},{5,4},{6,7},{7,6}} | collective-permute-start | bytes 393224 | tf_op jit(solution)/shard_map/ppermute | solution.py:475
  33.2 2.3 %collective-permute-start.2 = (bf16[64,1024]{1,0:T(8,128)(2,1)S(1)}, bf16[64,1024]{1,0:T(8,128)(2,1)S(1)}, u32[]{:S(2)}, u32[]{:S(2)}) collective-permute-start(bf16[64,1024]{1,0:T(8,128)(2,1)S(1)} %collective-permute-done.1.b2.token), channel_id=1, source_target_pairs={{0,1},{1,0},{2,3},{3,2},{4,5},{5,4},{6,7},{7,6}} | collective-permute-start | bytes 393224 | tf_op jit(solution)/shard_map/ppermute | solution.py:476

commit v5 on v4

--- a/solution.py
+++ b/solution.py
@@ -22,10 +22,9 @@
 OUT = 16
 NOUT = ROWS // OUT
 BLK = 1024
-SPLIT = 5
+SPLIT = 6
 AHEAD = 4
 SHARED = 3
-RELAY = 2
 NOWN = 8 - SHARED
 NW = NOWN + 1
 DIST = 1
@@ -42,8 +41,9 @@
     sp = lax.axis_index('sp')
     x, c = sp // 2, sp % 2
     sib = 2 * x + (1 - c)
-    xp = 2 * (1 - x) + c
-    diag = 2 * (1 - x) + 1 - c
+    xp = 2 * (1 - x) + 1 - c
+    diag = 2 * (1 - x) + c
+    part = (x + c) % 2
     first_pos = sp * SEQ
 
     def remote(src, dst, ss, rs, peer):
@@ -98,11 +98,11 @@
     vl_cp.start()
 
     barrier = pltpu.get_barrier_semaphore()
-    for peer in (sib, xp, diag):
+    for peer in (sib, xp):
         pl.semaphore_signal(barrier, inc=1, device_id={'sp': peer}, device_id_type=MESH)
 
     hid_cp.wait()
-    pl.semaphore_wait(barrier, 3)
+    pl.semaphore_wait(barrier, 2)
 
     def spread(slot, q):
         for h in range(2):
@@ -110,57 +110,44 @@
 
     def slot(i, chip, core):
         h = head(i, chip)
-        return 8 * (h // 4) + 4 * core + h % 4
-
-    def q_core(i):
-        return remote(qsend.at[i], qrecv.at[i], qs.at[0], qr.at[0], sib)
+        return 8 * ((core + h // 4) % 2) + 4 * core + h % 4
+
+    def q_core(i, kind):
+        return remote(qsend.at[i], qrecv.at[i], qs.at[0], qr.at[kind], sib)
 
     def q_chip(i):
         return remote(qsend.at[i], qchip.at[i], qxs.at[0], qxr.at[i], xp)
 
-    def q_far(i):
-        return remote(qsend.at[i], qrecv.at[NW + i], qxs.at[0], qrr.at[0], diag)
-
     def q_relay(i):
         return remote(qchip.at[i], qrecv.at[NW + i], qrs.at[0], qrr.at[0], sib)
 
-    def project(i):
+    def project(i, kind):
         pltpu.make_async_copy(wk_hbm, wbuf.at[i], s_w.at[i % AHEAD]).wait()
         start_w(i + AHEAD)
         res = jnp.dot(hid[...], wbuf[i], preferred_element_type=F32).astype(BF16)
         qsend[i] = res
-        q_core(i).start()
+        q_core(i, kind).start()
         return res.astype(F32)
 
     def head_step(i, _):
-        res = project(i)
+        res = project(i, 0)
 
         @pl.when(i < SHARED)
         def _():
             q_chip(i).start()
-
-        @pl.when((i >= RELAY) & (i < SHARED))
-        def _():
-            q_far(i).start()
 
         spread(slot(i, x, c), res)
         return 0
 
     lax.fori_loop(0, NOWN, head_step, 0)
-    for g in range(NCH + NW - AHEAD - NW, NCH):
-        if g + NW >= NW + AHEAD:
-            k_cp(g).start()
-            v_cp(g).start()
-    kvn[c] = project(NOWN)
-    for i in range(RELAY):
+    kvn[c] = project(NOWN, 1)
+    for i in range(SHARED):
         q_chip(i).wait_recv()
         q_relay(i).start()
     for i in range(SHARED):
-        if i >= RELAY:
-            q_chip(i).wait_recv()
-        spread(slot(i, 1 - x, c), qchip[i].astype(F32))
-    remote(qsend, qrecv.at[pl.ds(0, NW)], qs.at[0], qr.at[0], sib).wait_recv()
-    kvn[1 - c] = qrecv[NOWN].astype(F32)
+        spread(slot(i, 1 - x, 1 - c), qchip[i].astype(F32))
+    heads = pl.ds(0, NOWN)
+    remote(qsend.at[heads], qrecv.at[heads], qs.at[0], qr.at[0], sib).wait_recv()
 
     def take_head(i, _):
         spread(slot(i, x, 1 - c), qrecv[i].astype(F32))
@@ -169,7 +156,9 @@
     lax.fori_loop(0, NOWN, take_head, 0)
     remote(qchip, qrecv.at[pl.ds(NW, SHARED)], qrs.at[0], qrr.at[0], sib).wait_recv()
     for i in range(SHARED):
-        spread(slot(i, 1 - x, 1 - c), qrecv[NW + i].astype(F32))
+        spread(slot(i, 1 - x, c), qrecv[NW + i].astype(F32))
+    q_core(NOWN, 1).wait_recv()
+    kvn[1 - c] = qrecv[NOWN].astype(F32)
     wp_cp.wait()
     vl_cp.wait()
 
@@ -241,13 +230,13 @@
                         acc[core, ch, xd * CR + p * 8:xd * CR + p * 8 + 8, :] = os[xd]
 
     def d2d(ch):
-        return remote(acc.at[1 - c, ch], racc1.at[ch], a1s.at[0], a1r.at[ch], sib)
+        return remote(acc.at[1 - part, ch], racc1.at[ch], a1s.at[0], a1r.at[ch], sib)
 
     def xlink(ch):
         sums = pl.ds(pl.multiple_of((1 - x) * CR, 8), CR)
         lanes = pl.ds(pl.multiple_of((1 - x) * 128, 128), 128)
-        return (remote(acc.at[c, ch, sums], racc2.at[ch], a2s.at[0], a2r.at[ch], xp),
-                remote(acc.at[c, ch, pl.ds(2 * CR, 8), lanes], rml2.at[ch], m2s.at[0], m2r.at[ch], xp))
+        return (remote(acc.at[part, ch, sums], racc2.at[ch], a2s.at[0], a2r.at[ch], xp),
+                remote(acc.at[part, ch, pl.ds(2 * CR, 8), lanes], rml2.at[ch], m2s.at[0], m2r.at[ch], xp))
 
     def scales(mla, mlb):
         top = jnp.maximum(mla, mlb)
@@ -259,11 +248,11 @@
         d2d(ch).wait_recv()
         for xd in range(2):
             lanes = slice(xd * 128, xd * 128 + 128)
-            top, sa, sb, total = scales(acc[c, ch, 2 * CR:, lanes], racc1[ch, 2 * CR:, lanes])
-            acc[c, ch, 2 * CR:, lanes] = jnp.where(lane1 < 64, top, total)
+            top, sa, sb, total = scales(acc[part, ch, 2 * CR:, lanes], racc1[ch, 2 * CR:, lanes])
+            acc[part, ch, 2 * CR:, lanes] = jnp.where(lane1 < 64, top, total)
             for p in range(NPAIR):
                 r = slice(xd * CR + p * 8, xd * CR + p * 8 + 8)
-                acc[c, ch, r, :] = acc[c, ch, r, :] * sa[:, p:p + 1] + racc1[ch, r, :] * sb[:, p:p + 1]
+                acc[part, ch, r, :] = acc[part, ch, r, :] * sa[:, p:p + 1] + racc1[ch, r, :] * sb[:, p:p + 1]
         for desc in xlink(ch):
             desc.start()
 
@@ -271,12 +260,12 @@
         for desc in xlink(ch):
             desc.wait_recv()
         lanes = pl.ds(pl.multiple_of(x * 128, 128), 128)
-        top, sa, sb, total = scales(acc[c, ch, 2 * CR:, lanes], rml2[ch])
+        top, sa, sb, total = scales(acc[part, ch, 2 * CR:, lanes], rml2[ch])
         inv = pltpu.roll(1.0 / jnp.where(lane1 < 64, 1.0, total), 64, 1)
         sa, sb = sa * inv, sb * inv
         for p in range(NPAIR):
             mine = pl.ds(pl.multiple_of(x * CR + p * 8, 8), 8)
-            o = acc[c, ch, mine, :] * sa[:, p:p + 1] + racc2[ch, p * 8:p * 8 + 8, :] * sb[:, p:p + 1]
+            o = acc[part, ch, mine, :] * sa[:, p:p + 1] + racc2[ch, p * 8:p * 8 + 8, :] * sb[:, p:p + 1]
             for h in range(2):
                 osum[h, pl.ds(pl.multiple_of(ch * CR + p * 8, 8), 8), :] = o[:, h * 128:(h + 1) * 128]
 
@@ -348,10 +337,9 @@
     send_far(NOUT - 1)
 
     remote(qsend, qrecv.at[pl.ds(0, NW)], qs.at[0], qr.at[0], sib).wait_send()
-    n_far = 2 * SHARED - RELAY
-    remote(qrecv.at[pl.ds(0, n_far)], qrecv.at[pl.ds(0, n_far)], qxs.at[0], qxr.at[0], xp).wait_send()
-    remote(qchip.at[pl.ds(0, RELAY)], qrecv.at[pl.ds(0, RELAY)], qrs.at[0], qrr.at[0], sib).wait_send()
-    remote(acc.at[1 - c], racc1, a1s.at[0], a1r.at[0], sib).wait_send()
+    remote(qchip, qchip, qxs.at[0], qxr.at[0], xp).wait_send()
+    remote(qchip, qrecv.at[pl.ds(NW, SHARED)], qrs.at[0], qrr.at[0], sib).wait_send()
+    remote(acc.at[1 - part], racc1, a1s.at[0], a1r.at[0], sib).wait_send()
     remote(racc2, racc2, a2s.at[0], a2r.at[0], xp).wait_send()
     remote(rml2, rml2, m2s.at[0], m2r.at[0], xp).wait_send()
     remote(px, rx, f_s.at[0], f_r.at[0], sib).wait_send()
@@ -409,7 +397,7 @@
     x, c = sp // 2, sp % 2
     copies = []
     for i, ref in enumerate((b0, b1, b2, b3)):
-        j = 2 * (x if i < 2 else 1 - x) + (c if i % 2 == 0 else 1 - c)
+        j = (sp, 2 * x + 1 - c, 3 - sp, 2 * (1 - x) + c)[i]
         cols = pl.ds(pl.multiple_of(j * BLK, BLK), BLK)
         copies.append(pltpu.make_async_copy(ref, out.at[:, cols], sems.at[i]))
     for cp in copies:
@@ -461,7 +449,7 @@
                 pltpu.VMEM((ROWS, BLK), F32),
                 pltpu.VMEM((ROWS, BLK), F32),
                 dma((3,)), dma((AHEAD,)), dma((NCH,)), dma((NCH,)), dma((1,)),
-                dma((1,)), dma((1,)), dma((1,)), dma((SHARED,)), dma((1,)), dma((1,)),
+                dma((1,)), dma((2,)), dma((1,)), dma((SHARED,)), dma((1,)), dma((1,)),
                 dma((1,)), dma((NCH,)), dma((1,)), dma((NCH,)), dma((1,)), dma((NCH,)),
                 dma((1,)), dma((NOUT,)), dma((1,)), dma((1,)), dma((1,)), dma((1,)),
             ],
@@ -471,7 +459,7 @@
         )(*args)
         anywhere = pl.BlockSpec(memory_space=pltpu.HBM)
         near = [(i, i ^ 1) for i in range(4)]
-        chip = lax.ppermute(out, 'sp', [(i, i ^ 2) for i in range(4)])
+        chip = lax.ppermute(out, 'sp', [(i, 3 - i) for i in range(4)])
         core = lax.ppermute(out, 'sp', near)
         far = lax.ppermute(chip, 'sp', near)
         k_full, v_full, k_new, v_new = pl.pallas_call(

time: 36.4 us -> 35.6 us (0.978)
  starting transfers between devices: 1.43 us -> 0.9 us
    ppermute x1, starting transfers between devices: 0.9 us -> 0.37 us  [local_step(): chip = lax.ppermute(out, 'sp', [(i, 3 - i) for i in range(4)])]
    ppermute x1, starting transfers between devices: 0.01 us -> 0.4 us  [local_step(): core = lax.ppermute(out, 'sp', near)]
    ppermute x1, starting transfers between devices: 0.52 us -> 0.14 us  [local_step(): far = lax.ppermute(chip, 'sp', near)]
where the time goes in v5:
time: 35.6 us; the launch traced here: 35.5 us
  Pallas kernels  33.9 us (95%)
  starting transfers between devices  0.9 us (3%)
  between operations  0.68 us (2%)
    pallas_call x1, Pallas kernels, local_step(): pl.pallas_call(step_kernel, out_shape=[pltpu.VMEM((ROWS, BLK), BF16), plt...  26.2 us
    pallas_call x1, Pallas kernels, local_step(): pl.pallas_call(cache_kernel, out_shape=[pltpu.VMEM(flat, BF16), pltpu.VME...  5.5 us
    pallas_call x1, Pallas kernels, local_step(): pl.pallas_call(rest_kernel, out_shape=pltpu.HBM(flat, BF16), in_specs=[vm...  1.38 us
    pallas_call x1, Pallas kernels, local_step(): pl.pallas_call(join_kernel, out_shape=pltpu.HBM((ROWS, DIM), BF16), in_sp...  0.83 us
  transfers between devices with their start and end apart: 3, of which 0 were waited for; matrix products, arithmetic and copies ran while one was open for 0% of the time, Pallas kernels for 19%

profile of v5, /device:TPU:0, one launch (start us, length us, event | category | flops | bytes accessed | tf_op | source)
XLA Modules:
  0.0 35.5 jit_solution(16768569148211731943)
XLA Ops:
  0.6 26.2 %decode_step.1 = (bf16[64,1024]{1,0:T(8,128)(2,1)S(1)}, bf16[16384,256]{1,0:T(8,128)(2,1)S(1)}, bf16[16384,256]{1,0:T(8,128)(2,1)S(1)}, f32[2,64,256]{2,1,0:T(8,128)S(1)}, s32[64]{0:T(128)S(4)}) custom-call(bf16[64,4096]{1,0:T(8,128)(2,1)} %hid_hbm.1, bf16[4096,4096]{1,0:T(8,128)(2,1)} %wq_hbm.1, bf16[4096,256]{1,0:T(8,128)(2,1)} %wk_hbm.1, ...), custom_call_target="tpu_custom_call" | custom-call | tf_op jit(solution)/shard_map/decode_step/pallas_call | solution.py:421
  26.9 0.4 %collective-permute-start.1 = (bf16[64,1024]{1,0:T(8,128)(2,1)S(1)}, bf16[64,1024]{1,0:T(8,128)(2,1)S(1)}, u32[]{:S(2)}, u32[]{:S(2)}) collective-permute-start(bf16[64,1024]{1,0:T(8,128)(2,1)S(1)} %get-tuple-element.11.b0), channel_id=1, source_target_pairs={{0,3},{1,2},{2,1},{3,0},{4,7},{5,6},{6,5},{7,4}} | collective-permute-start | bytes 393224 | tf_op jit(solution)/shard_map/ppermute | solution.py:462
  27.2 0.4 %collective-permute-start = (bf16[64,1024]{1,0:T(8,128)(2,1)S(1)}, bf16[64,1024]{1,0:T(8,128)(2,1)S(1)}, u32[]{:S(2)}, u32[]{:S(2)}) collective-permute-start(bf16[64,1024]{1,0:T(8,128)(2,1)S(1)} %get-tuple-element.11.b0), channel_id=1, source_target_pairs={{0,1},{1,0},{2,3},{3,2},{4,5},{5,4},{6,7},{7,6}} | collective-permute-start | bytes 393224 | tf_op jit(solution)/shard_map/ppermute | solution.py:463
  27.6 5.5 %cache_update.1 = (bf16[16384,256]{1,0:T(8,128)(2,1)S(1)}, bf16[16384,256]{1,0:T(8,128)(2,1)S(1)}, bf16[16384,256]{1,0:T(8,128)(2,1)}, bf16[16384,256]{1,0:T(8,128)(2,1)}) custom-call(s32[64]{0:T(128)S(4)} %get-tuple-element.12.wp, f32[2,64,256]{2,1,0:T(8,128)S(1)} %get-tuple-element.13.kvn, ...), custom_call_target="tpu_custom_call", output_to_operand_aliasing={{0}: (2, {}), {1}: (3, {})} | custom-call | flops 8589934592 | bytes 33554432 | tf_op jit(solution)/shard_map/cache_update/pallas_call | solution.py:465
  33.1 0.0 collective-permute-done.1.b2.token
  33.1 0.1 collective-permute-start.2
  33.3 1.4 %cache_rest.1 = bf16[16384,256]{1,0:T(8,128)(2,1)} custom-call(bf16[16384,256]{1,0:T(8,128)(2,1)S(1)} %get-tuple-element.17.v_ref, bf16[64,1024]{1,0:T(8,128)(2,1)S(1)} %collective-permute-done.1.b2.token, bf16[16384,256]{1,0:T(8,128)(2,1)} %get-tuple-element.18.v_in), custom_call_target="tpu_custom_call", output_to_operand_aliasing={{}: (2, {})} | custom-call | flops 8589934592 | bytes 16777216 | tf_op jit(solution)/shard_map/cache_rest/pallas_call | solution.py:477
  34.7 0.0 collective-permute-done.b1
  34.7 0.0 collective-permute-done.2.b3
  34.7 0.8 %join.1 = bf16[64,4096]{1,0:T(8,128)(2,1)} custom-call(bf16[64,1024]{1,0:T(8,128)(2,1)S(1)} %get-tuple-element.11.b0, bf16[64,1024]{1,0:T(8,128)(2,1)S(1)} %collective-permute-done.b1, bf16[64,1024]{1,0:T(8,128)(2,1)S(1)} %collective-permute-done.1.b2.token, bf16[64,1024]{1,0:T(8,128)(2,1)S(1)} %collective-permute-done.2.b3), custom_call_target="tpu_custom_call" | custom-call | tf_op jit(solution)/shard_map/join/pallas_call | solution.py:489
Async XLA Ops:
  26.9 6.3 %collective-permute-start.1 = (bf16[64,1024]{1,0:T(8,128)(2,1)S(1)}, bf16[64,1024]{1,0:T(8,128)(2,1)S(1)}, u32[]{:S(2)}, u32[]{:S(2)}) collective-permute-start(bf16[64,1024]{1,0:T(8,128)(2,1)S(1)} %get-tuple-element.11.b0), channel_id=1, source_target_pairs={{0,3},{1,2},{2,1},{3,0},{4,7},{5,6},{6,5},{7,4}} | collective-permute-start | bytes 393224 | tf_op jit(solution)/shard_map/ppermute | solution.py:462
  27.2 7.4 %collective-permute-start = (bf16[64,1024]{1,0:T(8,128)(2,1)S(1)}, bf16[64,1024]{1,0:T(8,128)(2,1)S(1)}, u32[]{:S(2)}, u32[]{:S(2)}) collective-permute-start(bf16[64,1024]{1,0:T(8,128)(2,1)S(1)} %get-tuple-element.11.b0), channel_id=1, source_target_pairs={{0,1},{1,0},{2,3},{3,2},{4,5},{5,4},{6,7},{7,6}} | collective-permute-start | bytes 393224 | tf_op jit(solution)/shard_map/ppermute | solution.py:463
  33.1 1.5 %collective-permute-start.2 = (bf16[64,1024]{1,0:T(8,128)(2,1)S(1)}, bf16[64,1024]{1,0:T(8,128)(2,1)S(1)}, u32[]{:S(2)}, u32[]{:S(2)}) collective-permute-start(bf16[64,1024]{1,0:T(8,128)(2,1)S(1)} %collective-permute-done.1.b2.token), channel_id=1, source_target_pairs={{0,1},{1,0},{2,3},{3,2},{4,5},{5,4},{6,7},{7,6}} | collective-permute-start | bytes 393224 | tf_op jit(solution)/shard_map/ppermute | solution.py:464

commit v6 on v5

--- a/solution.py
+++ b/solution.py
@@ -140,12 +140,15 @@
         return 0
 
     lax.fori_loop(0, NOWN, head_step, 0)
-    kvn[c] = project(NOWN, 1)
-    for i in range(SHARED):
+    def take_shared(i):
         q_chip(i).wait_recv()
         q_relay(i).start()
-    for i in range(SHARED):
         spread(slot(i, 1 - x, 1 - c), qchip[i].astype(F32))
+
+    take_shared(0)
+    kvn[c] = project(NOWN, 1)
+    for i in range(1, SHARED):
+        take_shared(i)
     heads = pl.ds(0, NOWN)
     remote(qsend.at[heads], qrecv.at[heads], qs.at[0], qr.at[0], sib).wait_recv()
 
@@ -373,10 +376,12 @@
     for g in range(9):
         if g < 8:
             insert_rows(wp, kvn, first_pos, k_ref, 0, range(g, g + 1))
-            insert_rows(wp, kvn, first_pos, v_ref, 1, range(g, g + 1))
         if g >= 1:
             copies.append(copy_group(k_ref, k_out, sems.at[len(copies)], g - 1))
             copies[-1].start()
+        if g < 8:
+            insert_rows(wp, kvn, first_pos, v_ref, 1, range(g, g + 1))
+        if g >= 1:
             if g <= SPLIT:
                 copies.append(copy_group(v_ref, v_out, sems.at[len(copies)], g - 1))
                 copies[-1].start()

time: 35.6 us -> 35.6 us (level)
  no operation moved by 1% of the time
where the time goes in v6:
time: 35.6 us; the launch traced here: 35.5 us
  Pallas kernels  33.9 us (95%)
  starting transfers between devices  0.88 us (2%)
  between operations  0.68 us (2%)
    pallas_call x1, Pallas kernels, local_step(): pl.pallas_call(step_kernel, out_shape=[pltpu.VMEM((ROWS, BLK), BF16), plt...  26.2 us
    pallas_call x1, Pallas kernels, local_step(): pl.pallas_call(cache_kernel, out_shape=[pltpu.VMEM(flat, BF16), pltpu.VME...  5.46 us
    pallas_call x1, Pallas kernels, local_step(): pl.pallas_call(rest_kernel, out_shape=pltpu.HBM(flat, BF16), in_specs=[vm...  1.38 us
    pallas_call x1, Pallas kernels, local_step(): pl.pallas_call(join_kernel, out_shape=pltpu.HBM((ROWS, DIM), BF16), in_sp...  0.83 us
  transfers between devices with their start and end apart: 3, of which 0 were waited for; matrix products, arithmetic and copies ran while one was open for 0% of the time, Pallas kernels for 19%

profile of v6, /device:TPU:0, one launch (start us, length us, event | category | flops | bytes accessed | tf_op | source)
XLA Modules:
  0.0 35.5 jit_solution(180758362309046489)
XLA Ops:
  0.6 26.2 %decode_step.1 = (bf16[64,1024]{1,0:T(8,128)(2,1)S(1)}, bf16[16384,256]{1,0:T(8,128)(2,1)S(1)}, bf16[16384,256]{1,0:T(8,128)(2,1)S(1)}, f32[2,64,256]{2,1,0:T(8,128)S(1)}, s32[64]{0:T(128)S(4)}) custom-call(bf16[64,4096]{1,0:T(8,128)(2,1)} %hid_hbm.1, bf16[4096,4096]{1,0:T(8,128)(2,1)} %wq_hbm.1, bf16[4096,256]{1,0:T(8,128)(2,1)} %wk_hbm.1, ...), custom_call_target="tpu_custom_call" | custom-call | tf_op jit(solution)/shard_map/decode_step/pallas_call | solution.py:426
  26.9 0.3 collective-permute-start.1
  27.2 0.4 %collective-permute-start = (bf16[64,1024]{1,0:T(8,128)(2,1)S(1)}, bf16[64,1024]{1,0:T(8,128)(2,1)S(1)}, u32[]{:S(2)}, u32[]{:S(2)}) collective-permute-start(bf16[64,1024]{1,0:T(8,128)(2,1)S(1)} %get-tuple-element.11.b0), channel_id=1, source_target_pairs={{0,1},{1,0},{2,3},{3,2},{4,5},{5,4},{6,7},{7,6}} | collective-permute-start | bytes 393224 | tf_op jit(solution)/shard_map/ppermute | solution.py:468
  27.6 5.5 %cache_update.1 = (bf16[16384,256]{1,0:T(8,128)(2,1)S(1)}, bf16[16384,256]{1,0:T(8,128)(2,1)S(1)}, bf16[16384,256]{1,0:T(8,128)(2,1)}, bf16[16384,256]{1,0:T(8,128)(2,1)}) custom-call(s32[64]{0:T(128)S(4)} %get-tuple-element.12.wp, f32[2,64,256]{2,1,0:T(8,128)S(1)} %get-tuple-element.13.kvn, ...), custom_call_target="tpu_custom_call", output_to_operand_aliasing={{0}: (2, {}), {1}: (3, {})} | custom-call | flops 8589934592 | bytes 33554432 | tf_op jit(solution)/shard_map/cache_update/pallas_call | solution.py:470
  33.1 0.0 collective-permute-done.1.b2.token
  33.1 0.1 collective-permute-start.2
  33.2 1.4 %cache_rest.1 = bf16[16384,256]{1,0:T(8,128)(2,1)} custom-call(bf16[16384,256]{1,0:T(8,128)(2,1)S(1)} %get-tuple-element.17.v_ref, bf16[64,1024]{1,0:T(8,128)(2,1)S(1)} %collective-permute-done.1.b2.token, bf16[16384,256]{1,0:T(8,128)(2,1)} %get-tuple-element.18.v_in), custom_call_target="tpu_custom_call", output_to_operand_aliasing={{}: (2, {})} | custom-call | flops 8589934592 | bytes 16777216 | tf_op jit(solution)/shard_map/cache_rest/pallas_call | solution.py:482
  34.6 0.0 collective-permute-done.b1
  34.6 0.0 collective-permute-done.2.b3
  34.6 0.8 %join.1 = bf16[64,4096]{1,0:T(8,128)(2,1)} custom-call(bf16[64,1024]{1,0:T(8,128)(2,1)S(1)} %get-tuple-element.11.b0, bf16[64,1024]{1,0:T(8,128)(2,1)S(1)} %collective-permute-done.b1, bf16[64,1024]{1,0:T(8,128)(2,1)S(1)} %collective-permute-done.1.b2.token, bf16[64,1024]{1,0:T(8,128)(2,1)S(1)} %collective-permute-done.2.b3), custom_call_target="tpu_custom_call" | custom-call | tf_op jit(solution)/shard_map/join/pallas_call | solution.py:494
Async XLA Ops:
  26.9 6.2 %collective-permute-start.1 = (bf16[64,1024]{1,0:T(8,128)(2,1)S(1)}, bf16[64,1024]{1,0:T(8,128)(2,1)S(1)}, u32[]{:S(2)}, u32[]{:S(2)}) collective-permute-start(bf16[64,1024]{1,0:T(8,128)(2,1)S(1)} %get-tuple-element.11.b0), channel_id=1, source_target_pairs={{0,3},{1,2},{2,1},{3,0},{4,7},{5,6},{6,5},{7,4}} | collective-permute-start | bytes 393224 | tf_op jit(solution)/shard_map/ppermute | solution.py:467
  27.2 7.4 %collective-permute-start = (bf16[64,1024]{1,0:T(8,128)(2,1)S(1)}, bf16[64,1024]{1,0:T(8,128)(2,1)S(1)}, u32[]{:S(2)}, u32[]{:S(2)}) collective-permute-start(bf16[64,1024]{1,0:T(8,128)(2,1)S(1)} %get-tuple-element.11.b0), channel_id=1, source_target_pairs={{0,1},{1,0},{2,3},{3,2},{4,5},{5,4},{6,7},{7,6}} | collective-permute-start | bytes 393224 | tf_op jit(solution)/shard_map/ppermute | solution.py:468
  33.1 1.5 %collective-permute-start.2 = (bf16[64,1024]{1,0:T(8,128)(2,1)S(1)}, bf16[64,1024]{1,0:T(8,128)(2,1)S(1)}, u32[]{:S(2)}, u32[]{:S(2)}) collective-permute-start(bf16[64,1024]{1,0:T(8,128)(2,1)S(1)} %collective-permute-done.1.b2.token), channel_id=1, source_target_pairs={{0,1},{1,0},{2,3},{3,2},{4,5},{5,4},{6,7},{7,6}} | collective-permute-start | bytes 393224 | tf_op jit(solution)/shard_map/ppermute | solution.py:469

commit v7 on v6

--- a/solution.py
+++ b/solution.py
@@ -373,18 +373,16 @@
 def cache_kernel(wp, kvn, k_in, v_in, k_ref, v_ref, k_out, v_out, sems):
     first_pos = lax.axis_index('sp') * SEQ
     copies = []
-    for g in range(9):
-        if g < 8:
-            insert_rows(wp, kvn, first_pos, k_ref, 0, range(g, g + 1))
-        if g >= 1:
-            copies.append(copy_group(k_ref, k_out, sems.at[len(copies)], g - 1))
+    insert_rows(wp, kvn, first_pos, k_ref, 0, range(0, 1))
+    for g in range(8):
+        if g < 7:
+            insert_rows(wp, kvn, first_pos, k_ref, 0, range(g + 1, g + 2))
+        copies.append(copy_group(k_ref, k_out, sems.at[len(copies)], g))
+        copies[-1].start()
+        insert_rows(wp, kvn, first_pos, v_ref, 1, range(g, g + 1))
+        if 1 <= g <= SPLIT:
+            copies.append(copy_group(v_ref, v_out, sems.at[len(copies)], g - 1))
             copies[-1].start()
-        if g < 8:
-            insert_rows(wp, kvn, first_pos, v_ref, 1, range(g, g + 1))
-        if g >= 1:
-            if g <= SPLIT:
-                copies.append(copy_group(v_ref, v_out, sems.at[len(copies)], g - 1))
-                copies[-1].start()
     for cp in copies:
         cp.wait()
 

time: 35.6 us -> 35.5 us (level)
  no operation moved by 1% of the time
where the time goes in v7:
time: 35.5 us; the launch traced here: 35.4 us
  Pallas kernels  33.9 us (95%)
  starting transfers between devices  0.88 us (2%)
  between operations  0.68 us (2%)
    pallas_call x1, Pallas kernels, local_step(): pl.pallas_call(step_kernel, out_shape=[pltpu.VMEM((ROWS, BLK), BF16), plt...  26.2 us
    pallas_call x1, Pallas kernels, local_step(): pl.pallas_call(cache_kernel, out_shape=[pltpu.VMEM(flat, BF16), pltpu.VME...  5.43 us
    pallas_call x1, Pallas kernels, local_step(): pl.pallas_call(rest_kernel, out_shape=pltpu.HBM(flat, BF16), in_specs=[vm...  1.38 us
    pallas_call x1, Pallas kernels, local_step(): pl.pallas_call(join_kernel, out_shape=pltpu.HBM((ROWS, DIM), BF16), in_sp...  0.83 us
  transfers between devices with their start and end apart: 3, of which 0 were waited for; matrix products, arithmetic and copies ran while one was open for 0% of the time, Pallas kernels for 19%

profile of v7, /device:TPU:0, one launch (start us, length us, event | category | flops | bytes accessed | tf_op | source)
XLA Modules:
  0.0 35.4 jit_solution(12466410185841049200)
XLA Ops:
  0.6 26.2 %decode_step.1 = (bf16[64,1024]{1,0:T(8,128)(2,1)S(1)}, bf16[16384,256]{1,0:T(8,128)(2,1)S(1)}, bf16[16384,256]{1,0:T(8,128)(2,1)S(1)}, f32[2,64,256]{2,1,0:T(8,128)S(1)}, s32[64]{0:T(128)S(4)}) custom-call(bf16[64,4096]{1,0:T(8,128)(2,1)} %hid_hbm.1, bf16[4096,4096]{1,0:T(8,128)(2,1)} %wq_hbm.1, bf16[4096,256]{1,0:T(8,128)(2,1)} %wk_hbm.1, ...), custom_call_target="tpu_custom_call" | custom-call | tf_op jit(solution)/shard_map/decode_step/pallas_call | solution.py:424
  26.9 0.3 collective-permute-start.1
  27.2 0.4 %collective-permute-start = (bf16[64,1024]{1,0:T(8,128)(2,1)S(1)}, bf16[64,1024]{1,0:T(8,128)(2,1)S(1)}, u32[]{:S(2)}, u32[]{:S(2)}) collective-permute-start(bf16[64,1024]{1,0:T(8,128)(2,1)S(1)} %get-tuple-element.11.b0), channel_id=1, source_target_pairs={{0,1},{1,0},{2,3},{3,2},{4,5},{5,4},{6,7},{7,6}} | collective-permute-start | bytes 393224 | tf_op jit(solution)/shard_map/ppermute | solution.py:466
  27.6 5.4 %cache_update.1 = (bf16[16384,256]{1,0:T(8,128)(2,1)S(1)}, bf16[16384,256]{1,0:T(8,128)(2,1)S(1)}, bf16[16384,256]{1,0:T(8,128)(2,1)}, bf16[16384,256]{1,0:T(8,128)(2,1)}) custom-call(s32[64]{0:T(128)S(4)} %get-tuple-element.12.wp, f32[2,64,256]{2,1,0:T(8,128)S(1)} %get-tuple-element.13.kvn, ...), custom_call_target="tpu_custom_call", output_to_operand_aliasing={{0}: (2, {}), {1}: (3, {})} | custom-call | flops 8589934592 | bytes 33554432 | tf_op jit(solution)/shard_map/cache_update/pallas_call | solution.py:468
  33.0 0.0 collective-permute-done.1.b2.token
  33.0 0.1 collective-permute-start.2
  33.2 1.4 %cache_rest.1 = bf16[16384,256]{1,0:T(8,128)(2,1)} custom-call(bf16[16384,256]{1,0:T(8,128)(2,1)S(1)} %get-tuple-element.17.v_ref, bf16[64,1024]{1,0:T(8,128)(2,1)S(1)} %collective-permute-done.1.b2.token, bf16[16384,256]{1,0:T(8,128)(2,1)} %get-tuple-element.18.v_in), custom_call_target="tpu_custom_call", output_to_operand_aliasing={{}: (2, {})} | custom-call | flops 8589934592 | bytes 16777216 | tf_op jit(solution)/shard_map/cache_rest/pallas_call | solution.py:480
  34.6 0.0 collective-permute-done.b1
  34.6 0.0 collective-permute-done.2.b3
  34.6 0.8 %join.1 = bf16[64,4096]{1,0:T(8,128)(2,1)} custom-call(bf16[64,1024]{1,0:T(8,128)(2,1)S(1)} %get-tuple-element.11.b0, bf16[64,1024]{1,0:T(8,128)(2,1)S(1)} %collective-permute-done.b1, bf16[64,1024]{1,0:T(8,128)(2,1)S(1)} %collective-permute-done.1.b2.token, bf16[64,1024]{1,0:T(8,128)(2,1)S(1)} %collective-permute-done.2.b3), custom_call_target="tpu_custom_call" | custom-call | tf_op jit(solution)/shard_map/join/pallas_call | solution.py:492
Async XLA Ops:
  26.9 6.2 %collective-permute-start.1 = (bf16[64,1024]{1,0:T(8,128)(2,1)S(1)}, bf16[64,1024]{1,0:T(8,128)(2,1)S(1)}, u32[]{:S(2)}, u32[]{:S(2)}) collective-permute-start(bf16[64,1024]{1,0:T(8,128)(2,1)S(1)} %get-tuple-element.11.b0), channel_id=1, source_target_pairs={{0,3},{1,2},{2,1},{3,0},{4,7},{5,6},{6,5},{7,4}} | collective-permute-start | bytes 393224 | tf_op jit(solution)/shard_map/ppermute | solution.py:465
  27.2 7.4 %collective-permute-start = (bf16[64,1024]{1,0:T(8,128)(2,1)S(1)}, bf16[64,1024]{1,0:T(8,128)(2,1)S(1)}, u32[]{:S(2)}, u32[]{:S(2)}) collective-permute-start(bf16[64,1024]{1,0:T(8,128)(2,1)S(1)} %get-tuple-element.11.b0), channel_id=1, source_target_pairs={{0,1},{1,0},{2,3},{3,2},{4,5},{5,4},{6,7},{7,6}} | collective-permute-start | bytes 393224 | tf_op jit(solution)/shard_map/ppermute | solution.py:466
  33.0 1.5 %collective-permute-start.2 = (bf16[64,1024]{1,0:T(8,128)(2,1)S(1)}, bf16[64,1024]{1,0:T(8,128)(2,1)S(1)}, u32[]{:S(2)}, u32[]{:S(2)}) collective-permute-start(bf16[64,1024]{1,0:T(8,128)(2,1)S(1)} %collective-permute-done.1.b2.token), channel_id=1, source_target_pairs={{0,1},{1,0},{2,3},{3,2},{4,5},{5,4},{6,7},{7,6}} | collective-permute-start | bytes 393224 | tf_op jit(solution)/shard_map/ppermute | solution.py:467
